TPU v7x, 128 devices: a whole 4x4x4 slice. The times are simulated.
128 devices in a mesh: seq: 16 (over y, z), rep: 8 (over x, core).
Axes of the slice: x: 4, y: 4, z: 4, core: 2. Of those that a mesh axis runs over, the one named last changes fastest.
Arguments:
- head_out: bfloat16 [8, 8192, 4096], P('rep', 'seq'), may hold values from -6 to 6
- grad_out: bfloat16 [8, 8192, 3584], P('rep', 'seq'), may hold values from -6 to 6
- hash_codes: int32 [8, 16, 3584], P('rep'), may hold values from 0 to 511
- loss_mask: int32 [8192], P('seq'), may hold values 0 or 1
- query_ids: int32 [64], replicated, may hold values from 0 to 8191
Outputs:
- attribution: float32 [8192, 64], P(('seq', 'rep'))
All inputs are finite; a program needn't handle non-finite values. No bound on the sum of `loss_mask` on one device may be relied on, other than what follows from the above.
Results may differ from a plain program's by a relative error of at most 0.0025.
Values may be sent and summed in bfloat16 or wider, within the bound.
No kernel may reach another device: no remote copies, remote signals or barrier semaphores. Data moves between devices by JAX's collectives and lax.ppermute only.
A program may use at most 64 MiB of HBM per device.

v0:
```python
import functools
import math

import jax
import jax.numpy as jnp
from jax import lax
from jax.sharding import Mesh
from jax.sharding import PartitionSpec as P

REP = ("rep_0", "rep_1")
SEQ = ("seq_0", "seq_1")
SEQ_REP = ("seq_0", "seq_1", "rep_0", "rep_1")


ridge_shift = 0.25
norm_floor = 1e-06


def from_everyone(array, axis):
    copies = jnp.broadcast_to(array, (lax.axis_size(axis), *array.shape))
    return lax.all_to_all(copies, axis, split_axis=0, concat_axis=0, tiled=True)


def joined_along(blocks, dim):
    shape = list(blocks.shape[1:])
    shape[dim] *= blocks.shape[0]
    return jnp.moveaxis(blocks, 0, dim).reshape(shape)


def collect(array, axis, dim):
    blocks = from_everyone(array, axis)
    return joined_along(blocks, dim)


def in_blocks(array, dim, size):
    before, after = (array.shape[:dim], array.shape[dim + 1 :])
    return jnp.moveaxis(array.reshape(*before, size, -1, *after), dim, 0)


def sent_and_summed(array, axis, dim):
    blocks = in_blocks(array, dim, lax.axis_size(axis))
    arrived = lax.all_to_all(blocks, axis, split_axis=0, concat_axis=0, tiled=True)
    return arrived.sum(axis=0)


def by_axis(array, axes):
    return functools.reduce(lax.psum, axes, array)


def build_sketches(outputs, gradient, codes):
    head_count = codes.shape[0]
    sketch_width = outputs.shape[1] // head_count
    model_width = gradient.shape[1]
    sketch_scale = math.sqrt(sketch_width / model_width)
    columns = jnp.arange(sketch_width, dtype=jnp.int32)

    def one_head(head_index):
        head_codes = codes[head_index]
        bucket = head_codes % sketch_width
        sign_flip = 1 - 2 * (head_codes // sketch_width)
        count_table = jnp.where(bucket[:, None] == columns[None, :], sign_flip[:, None], 0).astype(
            jnp.bfloat16
        )
        counted = jnp.dot(gradient, count_table, preferred_element_type=jnp.float32)
        picked = lax.dynamic_slice_in_dim(
            outputs, head_index * sketch_width, sketch_width, 1
        ).astype(jnp.float32)
        return (picked * counted * sketch_scale).astype(jnp.bfloat16)

    return lax.map(one_head, jnp.arange(head_count, dtype=jnp.int32))


def solve_queries(gram_sum, chosen, token_count):
    sketch_width = gram_sum.shape[0]
    gram_sum = gram_sum / token_count + ridge_shift * jnp.eye(sketch_width, dtype=jnp.float32)
    factor = jnp.linalg.cholesky(gram_sum)
    return jax.scipy.linalg.cho_solve((factor, True), chosen.T).astype(jnp.bfloat16)


def on_device(head_out, grad_out, hash_codes, loss_mask, query_ids):
    sketches = build_sketches(head_out[0], grad_out[0], hash_codes[0])
    tok_rows = loss_mask.shape[0]
    out_rows = tok_rows // lax.axis_size(REP)
    regrouped = lax.all_to_all(sketches, SEQ, split_axis=0, concat_axis=1, tiled=True)
    mask_all = collect(loss_mask, SEQ, 0)
    token_count = jnp.sum(mask_all.astype(jnp.float32)) + 1.0
    mask_bf = mask_all.astype(jnp.bfloat16)
    sketch = regrouped[0]
    gram_sum = jnp.dot((sketch * mask_bf[:, None]).T, sketch, preferred_element_type=jnp.float32)
    chosen = sketch[query_ids].astype(jnp.float32)
    solved = solve_queries(gram_sum, chosen, token_count)
    score_sum = jnp.dot(sketch, solved, preferred_element_type=jnp.float32)
    partial_rows = sent_and_summed(score_sum, SEQ, 0)
    contrib = sent_and_summed(partial_rows, REP, 0)
    row_start = lax.axis_index(REP) * out_rows
    mask_rows = lax.dynamic_slice_in_dim(loss_mask, row_start, out_rows, 0).astype(jnp.float32)
    partial_value = jnp.sum(mask_rows[:, None] * contrib * contrib, 0)
    norm_sum = by_axis(partial_value, SEQ_REP) / token_count
    return contrib / jnp.sqrt(norm_sum + norm_floor)


def solution(mesh):
    torus = Mesh(mesh.devices.reshape(4, 4, 4, 2), ("seq_0", "seq_1", "rep_0", "rep_1"))
    in_specs = (P(REP, SEQ, None), P(REP, SEQ, None), P(REP, None, None), P(SEQ), P())
    out_specs = P(SEQ_REP, None)
    return jax.shard_map(
        on_device, mesh=torus, in_specs=in_specs, out_specs=out_specs, check_vma=False
    )
```

profile of v0, /device:TPU:0, one launch (start us, length us, event | category | flops | bytes accessed | tf_op | source)
XLA Modules:
  0.0 393.3 jit_solution(8680294653808130275)
XLA Ops:
  1.3 8.2 %all-to-all-start.1 = ((s32[16,1,512]{2,1,0:T(1,128)}), s32[16,1,512]{2,1,0:T(1,128)S(1)}, u32[]{:S(2)}, u32[]{:S(2)}) async-start(s32[16,1,512]{2,1,0:T(1,128)} %broadcast_in_dim.44), calls=%async_computation.1 | async-start | bytes 65536 | tf_op jit(solution)/shard_map/all_to_all | solution.py:21
  9.5 6.5 %copy.19 = bf16[1,512,4096]{1,2,0:T(8,128)(2,1)} copy(bf16[1,512,4096]{2,1,0:T(8,128)(2,1)} %param.7) | data formatting | bytes 8388608 | tf_op args[0]
  16.0 161.3 %while.15 = (s32[]{:T(128)}, bf16[16,512,256]{2,1,0:T(8,128)(2,1)}, s32[16]{0:T(128)S(1)}, bf16[512,4096]{0,1:T(8,128)(2,1)}, s32[16,3584]{1,0:T(8,128)}, /*inde...) while((s32[]{:T(128)}, bf16[16,512,256]{2,1,0:T(8,128)(2,1)}, ...), condition=%wide.region_1.2_spmd.clone, body=%wide.region_0.1_spmd.clone.sunk | while | flops 942876160 | bytes 5343953 | solution.py:70
  29.8 5.4 %fusion.57 = bf16[1,512,256]{1,2,0:T(8,128)(2,1)S(1)} fusion(bf16[512,3584]{1,0:T(8,128)(2,1)} %get-tuple-element.251, s32[3584]{0:T(1024)S(1)} %get-tuple-element.222, s32[3584]{0:T(1024)S(1)} %get-tuple-element.223, bf16[512,4096]{0,1:T(8,128)(2,1)} %get-tuple-element.249, s32[]{:T(128)S(6)} %select_n.92), kind=kOutput, calls=%fused_computation.14.clone.1 | convolution fusion | flops 942800896 | bytes 4222980 | tf_op jit(solution)/shard_map/while/body/eval_jaxpr/dot_general | solution.py:64
  39.9 5.4 %fusion.57 = bf16[1,512,256]{1,2,0:T(8,128)(2,1)S(1)} fusion(bf16[512,3584]{1,0:T(8,128)(2,1)} %get-tuple-element.251, s32[3584]{0:T(1024)S(1)} %get-tuple-element.222, s32[3584]{0:T(1024)S(1)} %get-tuple-element.223, bf16[512,4096]{0,1:T(8,128)(2,1)} %get-tuple-element.249, s32[]{:T(128)S(6)} %select_n.92), kind=kOutput, calls=%fused_computation.14.clone.1 | convolution fusion | flops 942800896 | bytes 4222980 | tf_op jit(solution)/shard_map/while/body/eval_jaxpr/dot_general | solution.py:64
  50.0 5.4 %fusion.57 = bf16[1,512,256]{1,2,0:T(8,128)(2,1)S(1)} fusion(bf16[512,3584]{1,0:T(8,128)(2,1)} %get-tuple-element.251, s32[3584]{0:T(1024)S(1)} %get-tuple-element.222, s32[3584]{0:T(1024)S(1)} %get-tuple-element.223, bf16[512,4096]{0,1:T(8,128)(2,1)} %get-tuple-element.249, s32[]{:T(128)S(6)} %select_n.92), kind=kOutput, calls=%fused_computation.14.clone.1 | convolution fusion | flops 942800896 | bytes 4222980 | tf_op jit(solution)/shard_map/while/body/eval_jaxpr/dot_general | solution.py:64
  60.1 5.4 %fusion.57 = bf16[1,512,256]{1,2,0:T(8,128)(2,1)S(1)} fusion(bf16[512,3584]{1,0:T(8,128)(2,1)} %get-tuple-element.251, s32[3584]{0:T(1024)S(1)} %get-tuple-element.222, s32[3584]{0:T(1024)S(1)} %get-tuple-element.223, bf16[512,4096]{0,1:T(8,128)(2,1)} %get-tuple-element.249, s32[]{:T(128)S(6)} %select_n.92), kind=kOutput, calls=%fused_computation.14.clone.1 | convolution fusion | flops 942800896 | bytes 4222980 | tf_op jit(solution)/shard_map/while/body/eval_jaxpr/dot_general | solution.py:64
  70.2 5.4 %fusion.57 = bf16[1,512,256]{1,2,0:T(8,128)(2,1)S(1)} fusion(bf16[512,3584]{1,0:T(8,128)(2,1)} %get-tuple-element.251, s32[3584]{0:T(1024)S(1)} %get-tuple-element.222, s32[3584]{0:T(1024)S(1)} %get-tuple-element.223, bf16[512,4096]{0,1:T(8,128)(2,1)} %get-tuple-element.249, s32[]{:T(128)S(6)} %select_n.92), kind=kOutput, calls=%fused_computation.14.clone.1 | convolution fusion | flops 942800896 | bytes 4222980 | tf_op jit(solution)/shard_map/while/body/eval_jaxpr/dot_general | solution.py:64
  90.3 5.4 %fusion.57 = bf16[1,512,256]{1,2,0:T(8,128)(2,1)S(1)} fusion(bf16[512,3584]{1,0:T(8,128)(2,1)} %get-tuple-element.251, s32[3584]{0:T(1024)S(1)} %get-tuple-element.222, s32[3584]{0:T(1024)S(1)} %get-tuple-element.223, bf16[512,4096]{0,1:T(8,128)(2,1)} %get-tuple-element.249, s32[]{:T(128)S(6)} %select_n.92), kind=kOutput, calls=%fused_computation.14.clone.1 | convolution fusion | flops 942800896 | bytes 4222980 | tf_op jit(solution)/shard_map/while/body/eval_jaxpr/dot_general | solution.py:64
  110.5 5.4 %fusion.57 = bf16[1,512,256]{1,2,0:T(8,128)(2,1)S(1)} fusion(bf16[512,3584]{1,0:T(8,128)(2,1)} %get-tuple-element.251, s32[3584]{0:T(1024)S(1)} %get-tuple-element.222, s32[3584]{0:T(1024)S(1)} %get-tuple-element.223, bf16[512,4096]{0,1:T(8,128)(2,1)} %get-tuple-element.249, s32[]{:T(128)S(6)} %select_n.92), kind=kOutput, calls=%fused_computation.14.clone.1 | convolution fusion | flops 942800896 | bytes 4222980 | tf_op jit(solution)/shard_map/while/body/eval_jaxpr/dot_general | solution.py:64
  140.8 5.4 %fusion.57 = bf16[1,512,256]{1,2,0:T(8,128)(2,1)S(1)} fusion(bf16[512,3584]{1,0:T(8,128)(2,1)} %get-tuple-element.251, s32[3584]{0:T(1024)S(1)} %get-tuple-element.222, s32[3584]{0:T(1024)S(1)} %get-tuple-element.223, bf16[512,4096]{0,1:T(8,128)(2,1)} %get-tuple-element.249, s32[]{:T(128)S(6)} %select_n.92), kind=kOutput, calls=%fused_computation.14.clone.1 | convolution fusion | flops 942800896 | bytes 4222980 | tf_op jit(solution)/shard_map/while/body/eval_jaxpr/dot_general | solution.py:64
  150.8 5.4 %fusion.57 = bf16[1,512,256]{1,2,0:T(8,128)(2,1)S(1)} fusion(bf16[512,3584]{1,0:T(8,128)(2,1)} %get-tuple-element.251, s32[3584]{0:T(1024)S(1)} %get-tuple-element.222, s32[3584]{0:T(1024)S(1)} %get-tuple-element.223, bf16[512,4096]{0,1:T(8,128)(2,1)} %get-tuple-element.249, s32[]{:T(128)S(6)} %select_n.92), kind=kOutput, calls=%fused_computation.14.clone.1 | convolution fusion | flops 942800896 | bytes 4222980 | tf_op jit(solution)/shard_map/while/body/eval_jaxpr/dot_general | solution.py:64
  160.9 5.4 %fusion.57 = bf16[1,512,256]{1,2,0:T(8,128)(2,1)S(1)} fusion(bf16[512,3584]{1,0:T(8,128)(2,1)} %get-tuple-element.251, s32[3584]{0:T(1024)S(1)} %get-tuple-element.222, s32[3584]{0:T(1024)S(1)} %get-tuple-element.223, bf16[512,4096]{0,1:T(8,128)(2,1)} %get-tuple-element.249, s32[]{:T(128)S(6)} %select_n.92), kind=kOutput, calls=%fused_computation.14.clone.1 | convolution fusion | flops 942800896 | bytes 4222980 | tf_op jit(solution)/shard_map/while/body/eval_jaxpr/dot_general | solution.py:64
  177.2 7.4 %all-to-all-start = ((bf16[16,512,256]{2,1,0:T(8,128)(2,1)}), bf16[16,512,256]{2,1,0:T(8,128)(2,1)}, u32[]{:S(2)}, u32[]{:S(2)}) async-start(bf16[16,512,256]{2,1,0:T(8,128)(2,1)} %get-tuple-element.97), calls=%async_computation | async-start | bytes 8388608 | tf_op jit(solution)/shard_map/all_to_all | solution.py:84
  185.9 53.1 %all-to-all-done = bf16[16,512,256]{2,1,0:T(8,128)(2,1)} async-done(((bf16[16,512,256]{2,1,0:T(8,128)(2,1)}), bf16[16,512,256]{2,1,0:T(8,128)(2,1)}, u32[]{:S(2)}, u32[]{:S(2)}) %all-to-all-start) | async-done | bytes 4194336 | tf_op jit(solution)/shard_map/all_to_all | solution.py:84
  239.0 6.0 %fusion.22 = f32[256,256]{1,0:T(8,128)S(1)} fusion(bf16[16,512,256]{2,1,0:T(8,128)(2,1)} %all-to-all-done, bf16[16,512]{1,0:T(8,128)(2,1)S(1)} %fusion.37, f32[]{:T(128)S(6)} %add.100), kind=kOutput, calls=%fused_computation.36 | convolution fusion | flops 1075904512 | bytes 4472836 | tf_op jit(solution)/shard_map/dot_general | solution.py:89
  245.2 11.7 %cholesky.49 = f32[128,128]{1,0:T(8,128)S(1)} custom-call(f32[128,128]{1,0:T(8,128)S(1)} %cholesky.115), custom_call_target="Cholesky" | custom-call | tf_op jit(solution)/shard_map/jit(cholesky)/cholesky | solution.py:76
  257.0 9.8 %custom-call.18 = f32[1,128,128]{1,2,0:T(8,128)S(1)} custom-call(f32[1,128,128]{2,1,0:T(8,128)S(1)} %get-tuple-element.147), custom_call_target="InvertDiagBlocksLowerTriangular" | custom-call | tf_op jit(solution)/shard_map/jit(cholesky)/cholesky | solution.py:76
  267.3 11.9 %cholesky.103 = f32[128,128]{1,0:T(8,128)S(1)} custom-call(f32[128,128]{1,0:T(8,128)S(1)} %convolution_subtract_fusion), custom_call_target="Cholesky" | custom-call | tf_op jit(solution)/shard_map/jit(cholesky)/cholesky | solution.py:76
  285.1 19.7 %custom-call.19 = f32[2,128,128]{1,2,0:T(8,128)S(1)} custom-call(f32[2,128,128]{2,1,0:T(8,128)S(1)} %get-tuple-element.105), custom_call_target="InvertDiagBlocksLowerTriangular" | custom-call | tf_op jit(solution)/shard_map/jit(_cho_solve)/triangular_solve | solution.py:77
  313.0 37.4 %all_to_all.25 = f32[16,512,64]{1,2,0:T(8,128)S(1)} all-to-all(f32[16,512,64]{1,2,0:T(8,128)S(1)} %fusion.34), channel_id=1, replica_groups=mesh['seq_0'=4,'seq_1'=4,'rep_0'=4,'rep_1'=2] {'seq_0','seq_1'}, dimensions={0} | all-to-all | bytes 4194304 | tf_op jit(solution)/shard_map/all_to_all | solution.py:42
  363.9 8.8 %psum.28 = f32[64]{0:T(128)S(1)} all-reduce(f32[64]{0:T(128)S(1)} %fusion.33), channel_id=1, replica_groups=mesh['seq_0'=4,'seq_1'=4,'rep_0'=4,'rep_1'=2] {'seq_0'}, use_global_device_ids=true, to_apply=%region_10.11 | all-reduce | flops 64 | bytes 512 | tf_op jit(solution)/shard_map/psum | solution.py:47
  372.8 8.3 %psum.29 = f32[64]{0:T(128)S(1)} all-reduce(f32[64]{0:T(128)S(1)} %psum.28), channel_id=1, replica_groups=mesh['seq_0'=4,'seq_1'=4,'rep_0'=4,'rep_1'=2] {'seq_1'}, use_global_device_ids=true, to_apply=%region_11.12 | all-reduce | flops 64 | bytes 512 | tf_op jit(solution)/shard_map/psum | solution.py:47
  381.1 8.9 %psum.30 = f32[64]{0:T(128)S(1)} all-reduce(f32[64]{0:T(128)S(1)} %psum.29), channel_id=1, replica_groups=mesh['seq_0'=4,'seq_1'=4,'rep_0'=4,'rep_1'=2] {'rep_0'}, use_global_device_ids=true, to_apply=%region_12.13 | all-reduce | flops 64 | bytes 512 | tf_op jit(solution)/shard_map/psum | solution.py:47
  (140 shorter events, 106.6 us)
Async XLA Ops:
  1.3 175.9 %all-to-all-start.1 = ((s32[16,1,512]{2,1,0:T(1,128)}), s32[16,1,512]{2,1,0:T(1,128)S(1)}, u32[]{:S(2)}, u32[]{:S(2)}) async-start(s32[16,1,512]{2,1,0:T(1,128)} %broadcast_in_dim.44), calls=%async_computation.1 | async-start | bytes 65536 | tf_op jit(solution)/shard_map/all_to_all | solution.py:21
  177.2 7.4 %copy-start = (s32[64]{0:T(128)S(1)}, s32[64]{0:T(128)}, u32[]{:S(2)}) copy-start(s32[64]{0:T(128)} %param.11) | copy-start | bytes 772
  177.2 61.8 %all-to-all-start = ((bf16[16,512,256]{2,1,0:T(8,128)(2,1)}), bf16[16,512,256]{2,1,0:T(8,128)(2,1)}, u32[]{:S(2)}, u32[]{:S(2)}) async-start(bf16[16,512,256]{2,1,0:T(8,128)(2,1)} %get-tuple-element.97), calls=%async_computation | async-start | bytes 8388608 | tf_op jit(solution)/shard_map/all_to_all | solution.py:84
  351.6 10.6 %all-to-all-start.3 = ((f32[8,1,4096]{2,1,0:T(1,128)}), f32[8,1,4096]{2,1,0:T(1,128)S(1)}, u32[]{:S(2)}, u32[]{:S(2)}) async-start(f32[8,1,4096]{2,1,0:T(1,128)} %reshape.141), calls=%async_computation.3 | async-start | bytes 262144 | tf_op jit(solution)/shard_map/all_to_all | solution.py:42
where the time goes:
time: 397 us; the launch traced here: 393 us
  matrix products  97.4 us (25%)
  blocking collectives  66 us (17%)
  waiting for transfers between devices  58.5 us (15%)
  other arithmetic  57 us (14%)
  local copies, waits for them, and re-layouts  55.3 us (14%)
  loops' own time  37 us (9%)
  starting transfers between devices  20.1 us (5%)
    dot_general x16, matrix products, one_head(): counted = jnp.dot(gradient, count_table, preferred_element_type=jnp.float32)  86.1 us
    all_to_all x1, waiting for transfers between devices, on_device(): lax.all_to_all(sketches, SEQ, split_axis=0, concat_axis=1, tiled=True)  53.1 us
    all_to_all x1, blocking collectives, sent_and_summed(): lax.all_to_all(blocks, axis, split_axis=0, concat_axis=0, tiled=True)  37.4 us
    another operation x1, loops' own time, build_sketches(): return lax.map(one_head, jnp.arange(head_count, dtype=jnp.int32))  37 us
    another operation x6, other arithmetic, solve_queries(): factor = jnp.linalg.cholesky(gram_sum)  34.2 us
    psum x4, blocking collectives, by_axis(): return functools.reduce(lax.psum, axes, array)  28.5 us
    another operation x3, other arithmetic, solve_queries(): jax.scipy.linalg.cho_solve((factor, True), chosen.T).astype(jnp.bfloat16)  19.7 us
    dynamic_slice x16, local copies, waits for them, and re-layouts, one_head(): head_codes = codes[head_index]  15.2 us
  transfers between devices with their start and end apart: 3, of which 2 were waited for; matrix products, arithmetic and copies ran while one was open for 34% of the time, Pallas kernels for 0%

commit v1 on v0

v1 whole, which is shorter than its diff:
```python
import functools
import math

import jax
import jax.numpy as jnp
from jax import lax
from jax.experimental import pallas as pl
from jax.experimental.pallas import tpu as pltpu
from jax.sharding import Mesh
from jax.sharding import PartitionSpec as P

REP = ("rep_0", "rep_1")
SEQ = ("seq_0", "seq_1")
SEQ_REP = ("seq_0", "seq_1", "rep_0", "rep_1")

RIDGE = 0.25
FLOOR = 1e-06
WIDTH = 256
HALF = 128
EXTRA = 16
F32 = jnp.float32
BF16 = jnp.bfloat16


def dot(a, b, ca, cb, precision=None):
    dims = (((ca,), (cb,)), ((), ()))
    return lax.dot_general(a, b, dims, preferred_element_type=F32, precision=precision)


def params(mib=48):
    return pltpu.CompilerParams(vmem_limit_bytes=mib * 2**20)


def sketch_kernel(scale, code_ref, grad_ref, out_ref, mask_ref, local_ref, sketch_ref, pack_ref):
    tokens, width = grad_ref.shape
    queries = local_ref.shape[0]
    codes = code_ref[0]
    bucket = jnp.broadcast_to((codes & (WIDTH - 1)).astype(jnp.int16), (WIDTH, width))
    sign = jnp.broadcast_to((1 - 2 * (codes >> 8)).astype(F32).astype(BF16), (WIDTH, width))
    row = lax.broadcasted_iota(jnp.int32, (WIDTH, width), 0).astype(jnp.int16)
    table = jnp.where(row == bucket, sign, jnp.zeros((), BF16))
    hashed = dot(grad_ref[...], table, 1, 1)
    sketch = (out_ref[...].astype(F32) * hashed * scale).astype(BF16)
    sketch_ref[...] = sketch

    mask = mask_ref[...]
    masked = (sketch.astype(F32) * mask).astype(BF16)
    gram = dot(masked, sketch, 0, 0)
    token = lax.broadcasted_iota(jnp.int32, (queries, tokens), 1)
    picks = jnp.where(token == local_ref[...], 1.0, 0.0).astype(BF16)
    chosen = dot(picks, sketch, 1, 0).astype(BF16)

    upper, lower = gram[:HALF, :HALF], gram[HALF:, HALF:]
    r = lax.broadcasted_iota(jnp.int32, (HALF, HALF), 0)
    c = lax.broadcasted_iota(jnp.int32, (HALF, HALF), 1)
    both = jnp.where(r >= c, upper, lower)
    diagonal = jnp.sum(jnp.where(r == c, lower, 0.0), 0, keepdims=True)
    row16 = lax.broadcasted_iota(jnp.int32, (EXTRA, HALF), 0)
    extra = jnp.where(row16 == 0, diagonal, jnp.where(row16 == 1, jnp.sum(mask), 0.0))

    def put(start, value):
        rows = value.shape[0]
        high = value.astype(BF16)
        pack_ref[0, start : start + rows, :] = high
        start += WIDTH + EXTRA
        pack_ref[0, start : start + rows, :] = (value - high.astype(F32)).astype(BF16)

    put(0, gram[:HALF, HALF:])
    put(HALF, both)
    put(WIDTH, extra)
    start = 2 * (WIDTH + EXTRA)
    pack_ref[0, start : start + queries, :] = chosen[:, :HALF]
    pack_ref[0, start + queries : start + 2 * queries, :] = chosen[:, HALF:]


def build_sketches(head_out, grad_out, codes, mask, local):
    heads, width = codes.shape
    tokens = grad_out.shape[0]
    queries = local.shape[0]
    rows = 2 * (WIDTH + EXTRA) + 2 * queries
    return pl.pallas_call(
        functools.partial(sketch_kernel, math.sqrt(WIDTH / width)),
        grid=(heads,),
        in_specs=[
            pl.BlockSpec((1, 1, width), lambda h: (h, 0, 0)),
            pl.BlockSpec((tokens, width), lambda h: (0, 0)),
            pl.BlockSpec((tokens, WIDTH), lambda h: (0, h)),
            pl.BlockSpec((tokens, 1), lambda h: (0, 0)),
            pl.BlockSpec((queries, 1), lambda h: (0, 0)),
        ],
        out_specs=[
            pl.BlockSpec((tokens, WIDTH), lambda h: (0, h)),
            pl.BlockSpec((1, rows, HALF), lambda h: (h, 0, 0)),
        ],
        out_shape=[
            jax.ShapeDtypeStruct((tokens, heads * WIDTH), BF16),
            jax.ShapeDtypeStruct((heads, rows, HALF), BF16),
        ],
        compiler_params=params(),
        name="sketch",
    )(codes[:, None, :], grad_out, head_out, mask, local)


def solve_kernel(pack_ref, solved_ref, count_ref, work_ref, answer_ref):
    sources = pack_ref.shape[0]
    queries = (pack_ref.shape[1] - 2 * (WIDTH + EXTRA)) // 2

    def add(start, rows):
        total = pack_ref[0, start : start + rows, :].astype(F32)
        for s in range(1, sources):
            total = total + pack_ref[s, start : start + rows, :].astype(F32)
        return total

    low = WIDTH + EXTRA
    side = add(0, HALF) + add(low, HALF)
    both = add(HALF, HALF) + add(low + HALF, HALF)
    extra = add(WIDTH, EXTRA) + add(low + WIDTH, EXTRA)
    left = add(2 * low, queries)
    right = add(2 * low + queries, queries)
    count = extra[1:2, :] + 1.0
    count_ref[...] = jnp.broadcast_to(count, count_ref.shape)

    r = lax.broadcasted_iota(jnp.int32, (HALF, HALF), 0)
    c = lax.broadcasted_iota(jnp.int32, (HALF, HALF), 1)
    flipped = both.T
    upper = jnp.where(r >= c, both, flipped)
    lower = jnp.where(r < c, both, jnp.where(r == c, extra[0:1, :], flipped))
    ridge = jnp.where(r == c, RIDGE, 0.0)
    work_ref[:HALF, :HALF] = upper / count + ridge
    work_ref[:HALF, HALF:] = side / count
    work_ref[HALF:WIDTH, :HALF] = side.T / count
    work_ref[HALF:WIDTH, HALF:] = lower / count + ridge
    work_ref[WIDTH:, :HALF] = left
    work_ref[WIDTH:, HALF:] = right

    gram = work_ref[:WIDTH, :]
    chosen = work_ref[WIDTH:, :]
    rr = lax.broadcasted_iota(jnp.int32, (WIDTH, WIDTH), 0)
    cc = lax.broadcasted_iota(jnp.int32, (WIDTH, WIDTH), 1)
    unit = rr == cc
    trace = jnp.sum(jnp.where(unit, gram, 0.0))
    step = trace / jnp.sum(gram * gram)
    e1 = jnp.where(unit, 1.0, 0.0) - step * gram
    e1b = e1.astype(BF16)
    e2 = dot(e1b, e1b, 1, 0)
    e2b = e2.astype(BF16)
    e4b = dot(e2b, e2b, 1, 0).astype(BF16)

    def rough(rhs):
        y = rhs * step
        for e in (e1b, e2b, e4b):
            y = y + dot(y.astype(BF16), e, 1, 0)
        return y

    y = rough(chosen)
    for _ in range(3):
        y = y + rough(chosen - dot(y, gram, 1, 0, lax.Precision.HIGHEST))
    answer_ref[...] = y
    residual = chosen - dot(y, gram, 1, 0, lax.Precision.HIGHEST)
    fine = jnp.sum(residual * residual) <= 1e-11 * jnp.sum(chosen * chosen)

    @pl.when(jnp.logical_not(fine))
    def _():
        lane = lax.broadcasted_iota(jnp.int32, work_ref.shape, 1)
        lane1 = lax.broadcasted_iota(jnp.int32, (1, WIDTH), 1)

        def pivot(k, carry):
            whole = work_ref[...]
            row = work_ref[pl.ds(k, 1), :]
            value = jnp.sum(jnp.where(lane1 == k, row, 0.0), 1, keepdims=True)
            column = jnp.sum(jnp.where(lane == k, whole, 0.0), 1, keepdims=True)
            factor = jnp.where(lane1 == k, value - 1.0, row) / value
            work_ref[...] = whole - column * factor
            return carry

        lax.fori_loop(0, WIDTH, pivot, 0)
        answer_ref[...] = work_ref[WIDTH:, :]

    solved = answer_ref[...].astype(BF16)
    for s in range(sources):
        solved_ref[s] = solved


def solve(packs):
    sources, rows, _ = packs.shape
    queries = (rows - 2 * (WIDTH + EXTRA)) // 2
    return pl.pallas_call(
        solve_kernel,
        out_shape=[
            jax.ShapeDtypeStruct((sources, queries, WIDTH), BF16),
            jax.ShapeDtypeStruct((8, HALF), F32),
        ],
        scratch_shapes=[
            pltpu.VMEM((WIDTH + queries, WIDTH), F32),
            pltpu.VMEM((queries, WIDTH), F32),
        ],
        compiler_params=params(),
        name="solve",
    )(packs)


def score_kernel(sketch_ref, solved_ref, part_ref):
    heads, queries, _ = solved_ref.shape
    owners = part_ref.shape[0]
    total = None
    for h in range(heads):
        part = dot(sketch_ref[:, h * WIDTH : (h + 1) * WIDTH], solved_ref[h], 1, 1)
        total = part if total is None else total + part
    size = total.shape[0] // owners
    for o in range(owners):
        block = total[o * size : (o + 1) * size]
        part_ref[o] = jnp.concatenate([block[: size // 2], block[size // 2 :]], 1)


def score(sketch, solved, owners):
    queries = solved.shape[1]
    size = sketch.shape[0] // owners
    return pl.pallas_call(
        score_kernel,
        out_shape=jax.ShapeDtypeStruct((owners, size // 2, 2 * queries), F32),
        compiler_params=params(),
        name="score",
    )(sketch, solved)


def square_kernel(part_ref, mask_ref, contrib_ref, square_ref):
    owners = part_ref.shape[0]
    total = part_ref[0]
    for o in range(1, owners):
        total = total + part_ref[o]
    contrib_ref[...] = total
    rows, queries = total.shape[0], total.shape[1] // 2
    mask = mask_ref[...]
    top = jnp.sum(mask[:rows] * total * total, 0, keepdims=True)
    end = jnp.sum(mask[rows:] * total * total, 0, keepdims=True)
    square = top[:, :queries] + end[:, queries:]
    square_ref[...] = jnp.concatenate([square, square], 1)


def squares(parts, mask):
    owners, rows, lanes = parts.shape
    return pl.pallas_call(
        square_kernel,
        out_shape=[
            jax.ShapeDtypeStruct((rows, lanes), F32),
            jax.ShapeDtypeStruct((1, lanes), F32),
        ],
        compiler_params=params(),
        name="squares",
    )(parts, mask)


def finish_kernel(contrib_ref, square_ref, count_ref, result_ref):
    total = jnp.sum(square_ref[...], axis=(0, 1))[None, :]
    root = jnp.sqrt(total / count_ref[0:1, :] + FLOOR)
    scaled = contrib_ref[...] / root
    rows, queries = scaled.shape[0], scaled.shape[1] // 2
    result_ref[:rows, :] = scaled[:, :queries]
    result_ref[rows:, :] = scaled[:, queries:]


def finish(contrib, gathered, count):
    rows, lanes = contrib.shape
    return pl.pallas_call(
        finish_kernel,
        out_shape=jax.ShapeDtypeStruct((2 * rows, lanes // 2), F32),
        compiler_params=params(),
        name="finish",
    )(contrib, gathered, count)


def exchange(array, axis):
    return lax.all_to_all(array, axis, split_axis=0, concat_axis=0, tiled=True)


def from_everyone(array, axis):
    return exchange(jnp.broadcast_to(array, (lax.axis_size(axis), *array.shape)), axis)


def on_device(head_out, grad_out, hash_codes, loss_mask, query_ids):
    tokens = loss_mask.shape[0]
    owners = lax.axis_size(REP)
    size = tokens // owners
    mask = loss_mask.astype(F32)[:, None]
    local = (query_ids - lax.axis_index(SEQ) * tokens)[:, None]
    own_mask = lax.dynamic_slice_in_dim(mask, lax.axis_index(REP) * size, size, 0)
    sketch, packs = build_sketches(head_out[0], grad_out[0], hash_codes[0], mask, local)
    solved, count = solve(exchange(packs, SEQ))
    parts = score(sketch, exchange(solved, SEQ), owners)
    contrib, square = squares(exchange(parts, REP), own_mask)
    square = from_everyone(square, REP).sum(0)
    return finish(contrib, from_everyone(square, SEQ), count)


def solution(mesh):
    torus = Mesh(mesh.devices.reshape(4, 4, 4, 2), SEQ_REP)
    in_specs = (P(REP, SEQ, None), P(REP, SEQ, None), P(REP, None, None), P(SEQ), P())
    out_specs = P(SEQ_REP, None)
    return jax.shard_map(
        on_device, mesh=torus, in_specs=in_specs, out_specs=out_specs, check_vma=False
    )
```

time: 397 us -> 155 us (0.39)
  matrix products: 97.4 us -> 0 us
  Pallas kernels: 0 us -> 65.9 us
  other arithmetic: 57 us -> 1.36 us
  local copies, waits for them, and re-layouts: 55.3 us -> 1.53 us
  waiting for transfers between devices: 58.5 us -> 5.93 us
  loops' own time: 37 us -> 0 us
  starting transfers between devices: 20.1 us -> 4.3 us
  blocking collectives: 66 us -> 76 us
    dot_general x18 -> x0, matrix products: 95.6 us -> none  [the longest x16 86.1 us: one_head(): counted = jnp.dot(gradient, count_table, preferred_element_type=jnp.float32)]
    pallas_call x0 -> x5, Pallas kernels: none -> 65.9 us  [the longest x1 35.4 us: solve(): pl.pallas_call(solve_kernel, out_shape=[jax.ShapeDtypeStruct((sources, qu...]
    another operation x9 -> x0, other arithmetic: 53.9 us -> none  [the longest x6 34.2 us: solve_queries(): factor = jnp.linalg.cholesky(gram_sum)]
    all_to_all x3 -> x1, waiting for transfers between devices: 58.5 us -> 5.93 us  [exchange(): return lax.all_to_all(array, axis, split_axis=0, concat_axis=0, tiled=True)]
    all_to_all x1 -> x4, blocking collectives: 37.4 us -> 76 us  [exchange(): return lax.all_to_all(array, axis, split_axis=0, concat_axis=0, tiled=True)]
    another operation x2 -> x0, loops' own time: 37 us -> none  [the longest x1 37 us: build_sketches(): return lax.map(one_head, jnp.arange(head_count, dtype=jnp.int32))]
    psum x4 -> x0, blocking collectives: 28.5 us -> none  [by_axis(): return functools.reduce(lax.psum, axes, array)]
    dynamic_slice x32 -> x2, local copies, waits for them, and re-layouts: 24 us -> 0.17 us  [on_device(): lax.dynamic_slice_in_dim(mask, lax.axis_index(REP) * size, size, 0)]
  transfers between devices with their start and end apart: 3 -> 1, of which waited for: 2 -> 1; matrix products, arithmetic and copies ran while one was open for 34% -> 0% of each run, Pallas kernels for 0% -> 0%
where the time goes in v1:
time: 155 us
  blocking collectives  76 us (49%)
  Pallas kernels  65.9 us (43%)
  waiting for transfers between devices  5.93 us (4%)
  starting transfers between devices  4.3 us (3%)
    all_to_all x4, blocking collectives, exchange(): return lax.all_to_all(array, axis, split_axis=0, concat_axis=0, tiled=True)  76 us
    pallas_call x1, Pallas kernels, solve(): pl.pallas_call(solve_kernel, out_shape=[jax.ShapeDtypeStruct((sources, qu...  35.4 us
    pallas_call x1, Pallas kernels, build_sketches(): pl.pallas_call(functools.partial(sketch_kernel, math.sqrt(WIDTH / width))...  27.6 us
    all_to_all x1, waiting for transfers between devices, exchange(): return lax.all_to_all(array, axis, split_axis=0, concat_axis=0, tiled=True)  5.93 us
    all_to_all x1, starting transfers between devices, exchange(): return lax.all_to_all(array, axis, split_axis=0, concat_axis=0, tiled=True)  4.3 us
  transfers between devices with their start and end apart: 1, of which 1 were waited for; matrix products, arithmetic and copies ran while one was open for 0% of the time, Pallas kernels for 0%

profile of v1, /device:TPU:0, one launch (start us, length us, event | category | flops | bytes accessed | tf_op | source)
XLA Modules:
  0.0 155.1 jit_solution(15205737988067054561)
XLA Ops:
  0.0 1.1 broadcast_in_dim_squeeze.3.code_ref
  1.1 0.7 convert_element_type.3
  1.8 0.1 copy.14.mask_ref
  1.9 0.7 subtract_bitcast_fusion
  2.6 0.1 copy.15.local_ref
  2.7 27.6 %sketch.1 = (bf16[512,4096]{1,0:T(8,128)(2,1)}, bf16[16,672,128]{2,1,0:T(8,128)(2,1)S(1)}) custom-call(s32[16,1,3584]{2,1,0:T(1,128)S(1)} %broadcast_in_dim_squeeze.3.code_ref, bf16[512,3584]{1,0:T(8,128)(2,1)} %bitcast.11, bf16[512,4096]{1,0:T(8,128)(2,1)} %bitcast.10, f32[512,1]{1,0:T(8,128)S(1)} %copy.14.mask_ref, s32[64,1]{1,0:T(8,128)S(1)} %copy.15.local_ref), custom_call_target="tpu_custom_call" | custom-call | tf_op jit(solution)/shard_map/sketch/pallas_call | solution.py:81
  30.3 0.0 copy-start
  30.3 43.8 %all_to_all.25.pack_ref = bf16[16,672,128]{2,1,0:T(8,128)(2,1)S(1)} all-to-all(bf16[16,672,128]{2,1,0:T(8,128)(2,1)S(1)} %get-tuple-element.12), channel_id=1, replica_groups=mesh['seq_0'=4,'seq_1'=4,'rep_0'=4,'rep_1'=2] {'seq_0','seq_1'}, dimensions={0} | all-to-all | bytes 5505024 | tf_op jit(solution)/shard_map/all_to_all | solution.py:273
  74.0 35.4 %solve.1 = (bf16[16,64,256]{2,1,0:T(8,128)(2,1)S(1)}, f32[8,128]{1,0:T(8,128)S(1)}) custom-call(bf16[16,672,128]{2,1,0:T(8,128)(2,1)S(1)} %all_to_all.25.pack_ref), custom_call_target="tpu_custom_call" | custom-call | tf_op jit(solution)/shard_map/solve/pallas_call | solution.py:187
  109.5 13.8 %all_to_all.26.solved_ref = bf16[16,64,256]{2,1,0:T(8,128)(2,1)S(1)} all-to-all(bf16[16,64,256]{2,1,0:T(8,128)(2,1)S(1)} %get-tuple-element.13), channel_id=1, replica_groups=mesh['seq_0'=4,'seq_1'=4,'rep_0'=4,'rep_1'=2] {'seq_0','seq_1'}, dimensions={0} | all-to-all | bytes 1048576 | tf_op jit(solution)/shard_map/all_to_all | solution.py:273
  123.3 0.0 copy-done
  123.3 1.9 %score.1 = f32[8,32,128]{2,1,0:T(8,128)} custom-call(bf16[512,4096]{1,0:T(8,128)(2,1)S(1)} %copy-done, bf16[16,64,256]{2,1,0:T(8,128)(2,1)S(1)} %all_to_all.26.solved_ref), custom_call_target="tpu_custom_call" | custom-call | tf_op jit(solution)/shard_map/score/pallas_call | solution.py:218
  125.2 4.3 %all-to-all-start.2 = ((f32[8,32,128]{2,1,0:T(8,128)}), f32[8,32,128]{2,1,0:T(8,128)S(1)}, u32[]{:S(2)}, u32[]{:S(2)}) async-start(f32[8,32,128]{2,1,0:T(8,128)} %score.1), calls=%async_computation.2 | async-start | bytes 262144 | tf_op jit(solution)/shard_map/all_to_all | solution.py:273
  129.5 0.1 dynamic-slice_bitcast_fusion
  129.6 0.1 copy.16.mask_ref
  129.7 5.9 %all-to-all-done.2.part_ref = f32[8,32,128]{2,1,0:T(8,128)S(1)} async-done(((f32[8,32,128]{2,1,0:T(8,128)}), f32[8,32,128]{2,1,0:T(8,128)S(1)}, u32[]{:S(2)}, u32[]{:S(2)}) %all-to-all-start.2) | async-done | bytes 131104 | tf_op jit(solution)/shard_map/all_to_all | solution.py:273
  135.6 0.2 squares.1
  135.9 7.6 %all_to_all.27 = f32[8,1,128]{2,1,0:T(1,128)S(1)} all-to-all(f32[8,1,128]{2,1,0:T(1,128)S(1)} %broadcast_in_dim.14), channel_id=1, replica_groups=mesh['seq_0'=4,'seq_1'=4,'rep_0'=4,'rep_1'=2] {'rep_0','rep_1'}, dimensions={0} | all-to-all | bytes 8192 | tf_op jit(solution)/shard_map/all_to_all | solution.py:273
  143.5 10.8 %all_to_all.28.square_ref = f32[16,1,128]{2,1,0:T(1,128)S(1)} all-to-all(f32[16,1,128]{2,1,0:T(1,128)S(1)} %broadcast_in_dim.15), channel_id=1, replica_groups=mesh['seq_0'=4,'seq_1'=4,'rep_0'=4,'rep_1'=2] {'seq_0','seq_1'}, dimensions={0} | all-to-all | bytes 16384 | tf_op jit(solution)/shard_map/all_to_all | solution.py:273
  154.4 0.7 finish.1
  (3 shorter events, 0.0 us)
Async XLA Ops:
  30.3 93.0 %copy-start = (bf16[512,4096]{1,0:T(8,128)(2,1)S(1)}, bf16[512,4096]{1,0:T(8,128)(2,1)}, u32[]{:S(2)}) copy-start(bf16[512,4096]{1,0:T(8,128)(2,1)} %get-tuple-element.11.sketch_ref) | copy-start | bytes 12582916
  125.2 10.4 %all-to-all-start.2 = ((f32[8,32,128]{2,1,0:T(8,128)}), f32[8,32,128]{2,1,0:T(8,128)S(1)}, u32[]{:S(2)}, u32[]{:S(2)}) async-start(f32[8,32,128]{2,1,0:T(8,128)} %score.1), calls=%async_computation.2 | async-start | bytes 262144 | tf_op jit(solution)/shard_map/all_to_all | solution.py:273

commit v2 on v1

--- a/solution.py
+++ b/solution.py
@@ -18,6 +18,7 @@
 WIDTH = 256
 HALF = 128
 EXTRA = 16
+TURNS = 12
 F32 = jnp.float32
 BF16 = jnp.bfloat16
 
@@ -31,79 +32,106 @@
     return pltpu.CompilerParams(vmem_limit_bytes=mib * 2**20)
 
 
-def sketch_kernel(scale, code_ref, grad_ref, out_ref, mask_ref, local_ref, sketch_ref, pack_ref):
+def sketch_kernel(scale, code_ref, grad_ref, out_ref, mask_ref, query_ref, sketch_ref, pack_ref,
+                  hashed_ref, picks_ref):
     tokens, width = grad_ref.shape
-    queries = local_ref.shape[0]
-    codes = code_ref[0]
-    bucket = jnp.broadcast_to((codes & (WIDTH - 1)).astype(jnp.int16), (WIDTH, width))
-    sign = jnp.broadcast_to((1 - 2 * (codes >> 8)).astype(F32).astype(BF16), (WIDTH, width))
-    row = lax.broadcasted_iota(jnp.int32, (WIDTH, width), 0).astype(jnp.int16)
-    table = jnp.where(row == bucket, sign, jnp.zeros((), BF16))
-    hashed = dot(grad_ref[...], table, 1, 1)
-    sketch = (out_ref[...].astype(F32) * hashed * scale).astype(BF16)
-    sketch_ref[...] = sketch
-
-    mask = mask_ref[...]
-    masked = (sketch.astype(F32) * mask).astype(BF16)
-    gram = dot(masked, sketch, 0, 0)
-    token = lax.broadcasted_iota(jnp.int32, (queries, tokens), 1)
-    picks = jnp.where(token == local_ref[...], 1.0, 0.0).astype(BF16)
-    chosen = dot(picks, sketch, 1, 0).astype(BF16)
-
-    upper, lower = gram[:HALF, :HALF], gram[HALF:, HALF:]
-    r = lax.broadcasted_iota(jnp.int32, (HALF, HALF), 0)
-    c = lax.broadcasted_iota(jnp.int32, (HALF, HALF), 1)
-    both = jnp.where(r >= c, upper, lower)
-    diagonal = jnp.sum(jnp.where(r == c, lower, 0.0), 0, keepdims=True)
-    row16 = lax.broadcasted_iota(jnp.int32, (EXTRA, HALF), 0)
-    extra = jnp.where(row16 == 0, diagonal, jnp.where(row16 == 1, jnp.sum(mask), 0.0))
-
-    def put(start, value):
-        rows = value.shape[0]
-        high = value.astype(BF16)
-        pack_ref[0, start : start + rows, :] = high
-        start += WIDTH + EXTRA
-        pack_ref[0, start : start + rows, :] = (value - high.astype(F32)).astype(BF16)
-
-    put(0, gram[:HALF, HALF:])
-    put(HALF, both)
-    put(WIDTH, extra)
-    start = 2 * (WIDTH + EXTRA)
-    pack_ref[0, start : start + queries, :] = chosen[:, :HALF]
-    pack_ref[0, start + queries : start + 2 * queries, :] = chosen[:, HALF:]
-
-
-def build_sketches(head_out, grad_out, codes, mask, local):
+    heads = code_ref.shape[0]
+    queries = query_ref.shape[1]
+    step = pl.program_id(0)
+
+    @pl.when(step == 0)
+    def _():
+        local = query_ref[...] - lax.axis_index(SEQ) * tokens
+        token = lax.broadcasted_iota(jnp.int32, (tokens, queries), 0)
+        picks_ref[...] = jnp.where(token == local, 1.0, 0.0).T.astype(BF16)
+        hashed_ref[...] = jnp.zeros_like(hashed_ref)
+
+    def hash_head():
+        codes = code_ref[pl.ds(step, 1), :]
+        bucket = jnp.broadcast_to((codes & (WIDTH - 1)).astype(jnp.int16), (WIDTH, width))
+        sign = jnp.broadcast_to((1 - 2 * (codes >> 8)).astype(F32).astype(BF16), (WIDTH, width))
+        row = lax.broadcasted_iota(jnp.int32, (WIDTH, width), 0).astype(jnp.int16)
+        table = jnp.where(row == bucket, sign, jnp.zeros((), BF16))
+        return dot(grad_ref[...], table, 1, 1)
+
+    def finish_head():
+        sketch = (out_ref[...].astype(F32) * hashed_ref[...] * scale).astype(BF16)
+        sketch_ref[...] = sketch
+        mask = mask_ref[...].astype(F32)
+        masked = sketch.T * mask.astype(BF16)
+        gram = dot(masked, sketch, 1, 0)
+        chosen = dot(picks_ref[...], sketch, 1, 0).astype(BF16)
+
+        upper, lower = gram[:HALF, :HALF], gram[HALF:, HALF:]
+        r = lax.broadcasted_iota(jnp.int32, (HALF, HALF), 0)
+        c = lax.broadcasted_iota(jnp.int32, (HALF, HALF), 1)
+        both = jnp.where(r >= c, upper, lower)
+        diagonal = jnp.sum(jnp.where(r == c, lower, 0.0), 0, keepdims=True)
+        pair = jnp.concatenate([diagonal, jnp.broadcast_to(jnp.sum(mask), (1, HALF))], 0)
+        high = pair.astype(BF16).astype(F32)
+        extra = jnp.concatenate([high, pair - high, jnp.zeros((EXTRA - 4, HALF), F32)], 0)
+
+        def put(start, value):
+            top = value.astype(BF16)
+            pack_ref[0, start : start + HALF, :] = top
+            start += WIDTH
+            pack_ref[0, start : start + HALF, :] = (value - top.astype(F32)).astype(BF16)
+
+        put(0, gram[:HALF, HALF:])
+        put(HALF, both)
+        start = 2 * WIDTH
+        pack_ref[0, start : start + queries, :] = chosen[:, :HALF]
+        start += queries
+        pack_ref[0, start : start + queries, :] = chosen[:, HALF:]
+        start += queries
+        pack_ref[0, start:, :] = extra.astype(BF16)
+
+    @pl.when(step < heads)
+    def _():
+        finish_head()
+        hashed_ref[...] = hash_head()
+
+    @pl.when(step == heads)
+    def _():
+        finish_head()
+
+
+def build_sketches(head_out, grad_out, codes, mask, query_ids):
     heads, width = codes.shape
     tokens = grad_out.shape[0]
-    queries = local.shape[0]
-    rows = 2 * (WIDTH + EXTRA) + 2 * queries
+    queries = query_ids.shape[0]
+    rows = 2 * WIDTH + 2 * queries + EXTRA
+    last = lambda h: jnp.maximum(h - 1, 0)
     return pl.pallas_call(
         functools.partial(sketch_kernel, math.sqrt(WIDTH / width)),
-        grid=(heads,),
+        grid=(heads + 1,),
         in_specs=[
-            pl.BlockSpec((1, 1, width), lambda h: (h, 0, 0)),
+            pl.BlockSpec((heads, width), lambda h: (0, 0)),
             pl.BlockSpec((tokens, width), lambda h: (0, 0)),
-            pl.BlockSpec((tokens, WIDTH), lambda h: (0, h)),
-            pl.BlockSpec((tokens, 1), lambda h: (0, 0)),
-            pl.BlockSpec((queries, 1), lambda h: (0, 0)),
+            pl.BlockSpec((tokens, WIDTH), lambda h: (0, last(h))),
+            pl.BlockSpec((1, tokens), lambda h: (0, 0)),
+            pl.BlockSpec((1, queries), lambda h: (0, 0)),
         ],
         out_specs=[
-            pl.BlockSpec((tokens, WIDTH), lambda h: (0, h)),
-            pl.BlockSpec((1, rows, HALF), lambda h: (h, 0, 0)),
+            pl.BlockSpec((tokens, WIDTH), lambda h: (0, last(h))),
+            pl.BlockSpec((1, rows, HALF), lambda h: (last(h), 0, 0)),
         ],
         out_shape=[
             jax.ShapeDtypeStruct((tokens, heads * WIDTH), BF16),
             jax.ShapeDtypeStruct((heads, rows, HALF), BF16),
         ],
+        scratch_shapes=[
+            pltpu.VMEM((tokens, WIDTH), F32),
+            pltpu.VMEM((queries, tokens), BF16),
+        ],
         compiler_params=params(),
         name="sketch",
-    )(codes[:, None, :], grad_out, head_out, mask, local)
+    )(codes, grad_out, head_out, mask[None, :], query_ids[None, :])
 
 
 def solve_kernel(pack_ref, solved_ref, count_ref, work_ref, answer_ref):
     sources = pack_ref.shape[0]
-    queries = (pack_ref.shape[1] - 2 * (WIDTH + EXTRA)) // 2
+    queries = (pack_ref.shape[1] - 2 * WIDTH - EXTRA) // 2
 
     def add(start, rows):
         total = pack_ref[0, start : start + rows, :].astype(F32)
@@ -111,12 +139,12 @@
             total = total + pack_ref[s, start : start + rows, :].astype(F32)
         return total
 
-    low = WIDTH + EXTRA
-    side = add(0, HALF) + add(low, HALF)
-    both = add(HALF, HALF) + add(low + HALF, HALF)
-    extra = add(WIDTH, EXTRA) + add(low + WIDTH, EXTRA)
-    left = add(2 * low, queries)
-    right = add(2 * low + queries, queries)
+    side = add(0, HALF) + add(WIDTH, HALF)
+    both = add(HALF, HALF) + add(WIDTH + HALF, HALF)
+    left = add(2 * WIDTH, queries)
+    right = add(2 * WIDTH + queries, queries)
+    extra = add(2 * WIDTH + 2 * queries, EXTRA)
+    extra = extra[0:2, :] + extra[2:4, :]
     count = extra[1:2, :] + 1.0
     count_ref[...] = jnp.broadcast_to(count, count_ref.shape)
 
@@ -138,26 +166,29 @@
     rr = lax.broadcasted_iota(jnp.int32, (WIDTH, WIDTH), 0)
     cc = lax.broadcasted_iota(jnp.int32, (WIDTH, WIDTH), 1)
     unit = rr == cc
-    trace = jnp.sum(jnp.where(unit, gram, 0.0))
-    step = trace / jnp.sum(gram * gram)
-    e1 = jnp.where(unit, 1.0, 0.0) - step * gram
-    e1b = e1.astype(BF16)
-    e2 = dot(e1b, e1b, 1, 0)
-    e2b = e2.astype(BF16)
+    scale = 1.0 / jnp.sum(jnp.where(unit, gram, 0.0), 0, keepdims=True)
+    e1b = (jnp.where(unit, 1.0, 0.0) - gram * scale).astype(BF16)
+    e2b = dot(e1b, e1b, 1, 0).astype(BF16)
     e4b = dot(e2b, e2b, 1, 0).astype(BF16)
-
-    def rough(rhs):
-        y = rhs * step
+    target = 1e-11 * jnp.sum(chosen * chosen)
+
+    def refine(state):
+        turn, answer, rest, _ = state
+        y = rest * scale
         for e in (e1b, e2b, e4b):
             y = y + dot(y.astype(BF16), e, 1, 0)
-        return y
-
-    y = rough(chosen)
-    for _ in range(3):
-        y = y + rough(chosen - dot(y, gram, 1, 0, lax.Precision.HIGHEST))
-    answer_ref[...] = y
-    residual = chosen - dot(y, gram, 1, 0, lax.Precision.HIGHEST)
-    fine = jnp.sum(residual * residual) <= 1e-11 * jnp.sum(chosen * chosen)
+        answer = answer + y
+        rest = chosen - dot(answer, gram, 1, 0, lax.Precision.HIGHEST)
+        return turn + 1, answer, rest, jnp.sum(rest * rest)
+
+    def unfinished(state):
+        turn, _, _, size = state
+        return jnp.logical_and(turn < TURNS, jnp.logical_not(size <= target))
+
+    start = (0, jnp.zeros_like(chosen), chosen, jnp.float32(jnp.inf))
+    _, answer, _, size = lax.while_loop(unfinished, refine, start)
+    answer_ref[...] = answer
+    fine = size <= target
 
     @pl.when(jnp.logical_not(fine))
     def _():
@@ -183,7 +214,7 @@
 
 def solve(packs):
     sources, rows, _ = packs.shape
-    queries = (rows - 2 * (WIDTH + EXTRA)) // 2
+    queries = (rows - 2 * WIDTH - EXTRA) // 2
     return pl.pallas_call(
         solve_kernel,
         out_shape=[
@@ -281,10 +312,9 @@
     tokens = loss_mask.shape[0]
     owners = lax.axis_size(REP)
     size = tokens // owners
-    mask = loss_mask.astype(F32)[:, None]
-    local = (query_ids - lax.axis_index(SEQ) * tokens)[:, None]
-    own_mask = lax.dynamic_slice_in_dim(mask, lax.axis_index(REP) * size, size, 0)
-    sketch, packs = build_sketches(head_out[0], grad_out[0], hash_codes[0], mask, local)
+    own_mask = lax.dynamic_slice_in_dim(loss_mask, lax.axis_index(REP) * size, size, 0)
+    own_mask = own_mask.astype(F32)[:, None]
+    sketch, packs = build_sketches(head_out[0], grad_out[0], hash_codes[0], loss_mask, query_ids)
     solved, count = solve(exchange(packs, SEQ))
     parts = score(sketch, exchange(solved, SEQ), owners)
     contrib, square = squares(exchange(parts, REP), own_mask)

time: 155 us -> 158 us (1.019)
  Pallas kernels: 65.9 us -> 69.4 us
    pallas_call x1, Pallas kernels: 35.4 us -> 42.2 us  [solve(): pl.pallas_call(solve_kernel, out_shape=[jax.ShapeDtypeStruct((sources, qu...]
    pallas_call x1, Pallas kernels: 27.6 us -> 24.3 us  [build_sketches(): pl.pallas_call(functools.partial(sketch_kernel, math.sqrt(WIDTH / width))...]
    unnamed x2 -> x8, local copies, waits for them, and re-layouts: 0.01 us -> 2.28 us
  transfers between devices with their start and end apart: 1 -> 1, of which waited for: 1 -> 1; matrix products, arithmetic and copies ran while one was open for 0% -> 1% of each run, Pallas kernels for 0% -> 0%
where the time goes in v2:
time: 158 us; the launch traced here: 157 us
  blocking collectives  75.3 us (48%)
  Pallas kernels  69.4 us (44%)
  waiting for transfers between devices  5.25 us (3%)
  starting transfers between devices  4.29 us (3%)
  local copies, waits for them, and re-layouts  2.39 us (2%)
    all_to_all x4, blocking collectives, exchange(): return lax.all_to_all(array, axis, split_axis=0, concat_axis=0, tiled=True)  75.3 us
    pallas_call x1, Pallas kernels, solve(): pl.pallas_call(solve_kernel, out_shape=[jax.ShapeDtypeStruct((sources, qu...  42.2 us
    pallas_call x1, Pallas kernels, build_sketches(): pl.pallas_call(functools.partial(sketch_kernel, math.sqrt(WIDTH / width))...  24.3 us
    all_to_all x1, waiting for transfers between devices, exchange(): return lax.all_to_all(array, axis, split_axis=0, concat_axis=0, tiled=True)  5.25 us
    all_to_all x1, starting transfers between devices, exchange(): return lax.all_to_all(array, axis, split_axis=0, concat_axis=0, tiled=True)  4.29 us
  transfers between devices with their start and end apart: 1, of which 1 were waited for; matrix products, arithmetic and copies ran while one was open for 1% of the time, Pallas kernels for 0%

profile of v2, /device:TPU:0, one launch (start us, length us, event | category | flops | bytes accessed | tf_op | source)
XLA Modules:
  0.0 157.5 jit_solution(11412913429232144713)
XLA Ops:
  0.0 0.0 copy-start.1
  0.0 0.9 copy-done.1
  0.9 0.0 copy-start.2
  0.9 0.7 copy-done.2
  1.6 0.0 copy-start.3
  1.6 0.7 copy-done.3
  2.3 24.3 %sketch.1 = (bf16[512,4096]{1,0:T(8,128)(2,1)}, bf16[16,656,128]{2,1,0:T(8,128)(2,1)S(1)}) custom-call(s32[16,3584]{1,0:T(8,128)S(1)} %bitcast.9, bf16[512,3584]{1,0:T(8,128)(2,1)} %bitcast.14, bf16[512,4096]{1,0:T(8,128)(2,1)} %bitcast.13, s32[1,512]{1,0:T(1,128)S(1)} %bitcast.10, s32[1,64]{1,0:T(1,128)S(1)} %bitcast.11), custom_call_target="tpu_custom_call" | custom-call | tf_op jit(solution)/shard_map/sketch/pallas_call | solution.py:105
  26.6 0.0 copy-start
  26.6 43.3 %all_to_all.25.pack_ref = bf16[16,656,128]{2,1,0:T(8,128)(2,1)S(1)} all-to-all(bf16[16,656,128]{2,1,0:T(8,128)(2,1)S(1)} %get-tuple-element.12), channel_id=1, replica_groups=mesh['seq_0'=4,'seq_1'=4,'rep_0'=4,'rep_1'=2] {'seq_0','seq_1'}, dimensions={0} | all-to-all | bytes 5373952 | tf_op jit(solution)/shard_map/all_to_all | solution.py:304
  69.8 42.2 %solve.1 = (bf16[16,64,256]{2,1,0:T(8,128)(2,1)S(1)}, f32[8,128]{1,0:T(8,128)S(1)}) custom-call(bf16[16,656,128]{2,1,0:T(8,128)(2,1)S(1)} %all_to_all.25.pack_ref), custom_call_target="tpu_custom_call" | custom-call | tf_op jit(solution)/shard_map/solve/pallas_call | solution.py:218
  112.1 13.6 %all_to_all.26.solved_ref = bf16[16,64,256]{2,1,0:T(8,128)(2,1)S(1)} all-to-all(bf16[16,64,256]{2,1,0:T(8,128)(2,1)S(1)} %get-tuple-element.13), channel_id=1, replica_groups=mesh['seq_0'=4,'seq_1'=4,'rep_0'=4,'rep_1'=2] {'seq_0','seq_1'}, dimensions={0} | all-to-all | bytes 1048576 | tf_op jit(solution)/shard_map/all_to_all | solution.py:304
  125.7 0.0 copy-done
  125.7 1.9 %score.1 = f32[8,32,128]{2,1,0:T(8,128)} custom-call(bf16[512,4096]{1,0:T(8,128)(2,1)S(1)} %copy-done, bf16[16,64,256]{2,1,0:T(8,128)(2,1)S(1)} %all_to_all.26.solved_ref), custom_call_target="tpu_custom_call" | custom-call | tf_op jit(solution)/shard_map/score/pallas_call | solution.py:249
  127.7 4.3 %all-to-all-start.2 = ((f32[8,32,128]{2,1,0:T(8,128)}), f32[8,32,128]{2,1,0:T(8,128)S(1)}, u32[]{:S(2)}, u32[]{:S(2)}) async-start(f32[8,32,128]{2,1,0:T(8,128)} %score.1), calls=%async_computation.2 | async-start | bytes 262144 | tf_op jit(solution)/shard_map/all_to_all | solution.py:304
  131.9 0.8 convert_bitcast_fusion
  132.7 0.1 copy.8.mask_ref
  132.8 5.2 %all-to-all-done.2.part_ref = f32[8,32,128]{2,1,0:T(8,128)S(1)} async-done(((f32[8,32,128]{2,1,0:T(8,128)}), f32[8,32,128]{2,1,0:T(8,128)S(1)}, u32[]{:S(2)}, u32[]{:S(2)}) %all-to-all-start.2) | async-done | bytes 131104 | tf_op jit(solution)/shard_map/all_to_all | solution.py:304
  138.0 0.2 squares.1
  138.3 7.6 %all_to_all.27 = f32[8,1,128]{2,1,0:T(1,128)S(1)} all-to-all(f32[8,1,128]{2,1,0:T(1,128)S(1)} %broadcast_in_dim.18), channel_id=1, replica_groups=mesh['seq_0'=4,'seq_1'=4,'rep_0'=4,'rep_1'=2] {'rep_0','rep_1'}, dimensions={0} | all-to-all | bytes 8192 | tf_op jit(solution)/shard_map/all_to_all | solution.py:304
  145.9 10.8 %all_to_all.28.square_ref = f32[16,1,128]{2,1,0:T(1,128)S(1)} all-to-all(f32[16,1,128]{2,1,0:T(1,128)S(1)} %broadcast_in_dim.19), channel_id=1, replica_groups=mesh['seq_0'=4,'seq_1'=4,'rep_0'=4,'rep_1'=2] {'seq_0','seq_1'}, dimensions={0} | all-to-all | bytes 16384 | tf_op jit(solution)/shard_map/all_to_all | solution.py:304
  156.8 0.7 finish.1
  (3 shorter events, 0.0 us)
Async XLA Ops:
  0.0 0.9 copy-start.1
  0.9 0.7 copy-start.2
  1.6 0.7 copy-start.3
  26.6 99.1 %copy-start = (bf16[512,4096]{1,0:T(8,128)(2,1)S(1)}, bf16[512,4096]{1,0:T(8,128)(2,1)}, u32[]{:S(2)}) copy-start(bf16[512,4096]{1,0:T(8,128)(2,1)} %get-tuple-element.11.sketch_ref) | copy-start | bytes 12582916
  127.7 10.4 %all-to-all-start.2 = ((f32[8,32,128]{2,1,0:T(8,128)}), f32[8,32,128]{2,1,0:T(8,128)S(1)}, u32[]{:S(2)}, u32[]{:S(2)}) async-start(f32[8,32,128]{2,1,0:T(8,128)} %score.1), calls=%async_computation.2 | async-start | bytes 262144 | tf_op jit(solution)/shard_map/all_to_all | solution.py:304

commit v3 on v2

--- a/solution.py
+++ b/solution.py
@@ -19,6 +19,7 @@
 HALF = 128
 EXTRA = 16
 TURNS = 12
+GROUP = 4
 F32 = jnp.float32
 BF16 = jnp.bfloat16
 
@@ -35,65 +36,68 @@
 def sketch_kernel(scale, code_ref, grad_ref, out_ref, mask_ref, query_ref, sketch_ref, pack_ref,
                   hashed_ref, picks_ref):
     tokens, width = grad_ref.shape
-    heads = code_ref.shape[0]
     queries = query_ref.shape[1]
+    group = pack_ref.shape[0]
+    steps = code_ref.shape[0] // group
     step = pl.program_id(0)
+
+    def hash_heads():
+        tables = []
+        for g in range(group):
+            codes = code_ref[pl.ds(step * group + g, 1), :]
+            bucket = jnp.broadcast_to((codes & (WIDTH - 1)).astype(jnp.int16), (WIDTH, width))
+            sign = jnp.broadcast_to((1 - 2 * (codes >> 8)).astype(F32).astype(BF16), (WIDTH, width))
+            row = lax.broadcasted_iota(jnp.int32, (WIDTH, width), 0).astype(jnp.int16)
+            tables.append(jnp.where(row == bucket, sign, jnp.zeros((), BF16)))
+        table = tables[0] if group == 1 else jnp.concatenate(tables, 0)
+        hashed_ref[...] = dot(grad_ref[...], table, 1, 1)
+
+    def finish_heads():
+        mask = mask_ref[...].astype(F32)
+        mask_total = jnp.broadcast_to(jnp.sum(mask), (1, HALF))
+        mask = mask.astype(BF16)
+        for g in range(group):
+            columns = slice(g * WIDTH, (g + 1) * WIDTH)
+            sketch = (out_ref[:, columns].astype(F32) * hashed_ref[:, columns] * scale).astype(BF16)
+            sketch_ref[:, columns] = sketch
+            gram = dot(sketch.T * mask, sketch, 1, 0)
+            chosen = dot(picks_ref[...], sketch, 1, 0).astype(BF16)
+
+            upper, lower = gram[:HALF, :HALF], gram[HALF:, HALF:]
+            r = lax.broadcasted_iota(jnp.int32, (HALF, HALF), 0)
+            c = lax.broadcasted_iota(jnp.int32, (HALF, HALF), 1)
+            both = jnp.where(r >= c, upper, lower)
+            diagonal = jnp.sum(jnp.where(r == c, lower, 0.0), 0, keepdims=True)
+            pair = jnp.concatenate([diagonal, mask_total], 0)
+            high = pair.astype(BF16).astype(F32)
+            extra = jnp.concatenate([high, pair - high, jnp.zeros((EXTRA - 4, HALF), F32)], 0)
+            for start, value in ((0, gram[:HALF, HALF:]), (HALF, both)):
+                top = value.astype(BF16)
+                pack_ref[g, start : start + HALF, :] = top
+                start += WIDTH
+                pack_ref[g, start : start + HALF, :] = (value - top.astype(F32)).astype(BF16)
+            start = 2 * WIDTH
+            pack_ref[g, start : start + queries, :] = chosen[:, :HALF]
+            start += queries
+            pack_ref[g, start : start + queries, :] = chosen[:, HALF:]
+            start += queries
+            pack_ref[g, start:, :] = extra.astype(BF16)
 
     @pl.when(step == 0)
     def _():
         local = query_ref[...] - lax.axis_index(SEQ) * tokens
         token = lax.broadcasted_iota(jnp.int32, (tokens, queries), 0)
         picks_ref[...] = jnp.where(token == local, 1.0, 0.0).T.astype(BF16)
-        hashed_ref[...] = jnp.zeros_like(hashed_ref)
-
-    def hash_head():
-        codes = code_ref[pl.ds(step, 1), :]
-        bucket = jnp.broadcast_to((codes & (WIDTH - 1)).astype(jnp.int16), (WIDTH, width))
-        sign = jnp.broadcast_to((1 - 2 * (codes >> 8)).astype(F32).astype(BF16), (WIDTH, width))
-        row = lax.broadcasted_iota(jnp.int32, (WIDTH, width), 0).astype(jnp.int16)
-        table = jnp.where(row == bucket, sign, jnp.zeros((), BF16))
-        return dot(grad_ref[...], table, 1, 1)
-
-    def finish_head():
-        sketch = (out_ref[...].astype(F32) * hashed_ref[...] * scale).astype(BF16)
-        sketch_ref[...] = sketch
-        mask = mask_ref[...].astype(F32)
-        masked = sketch.T * mask.astype(BF16)
-        gram = dot(masked, sketch, 1, 0)
-        chosen = dot(picks_ref[...], sketch, 1, 0).astype(BF16)
-
-        upper, lower = gram[:HALF, :HALF], gram[HALF:, HALF:]
-        r = lax.broadcasted_iota(jnp.int32, (HALF, HALF), 0)
-        c = lax.broadcasted_iota(jnp.int32, (HALF, HALF), 1)
-        both = jnp.where(r >= c, upper, lower)
-        diagonal = jnp.sum(jnp.where(r == c, lower, 0.0), 0, keepdims=True)
-        pair = jnp.concatenate([diagonal, jnp.broadcast_to(jnp.sum(mask), (1, HALF))], 0)
-        high = pair.astype(BF16).astype(F32)
-        extra = jnp.concatenate([high, pair - high, jnp.zeros((EXTRA - 4, HALF), F32)], 0)
-
-        def put(start, value):
-            top = value.astype(BF16)
-            pack_ref[0, start : start + HALF, :] = top
-            start += WIDTH
-            pack_ref[0, start : start + HALF, :] = (value - top.astype(F32)).astype(BF16)
-
-        put(0, gram[:HALF, HALF:])
-        put(HALF, both)
-        start = 2 * WIDTH
-        pack_ref[0, start : start + queries, :] = chosen[:, :HALF]
-        start += queries
-        pack_ref[0, start : start + queries, :] = chosen[:, HALF:]
-        start += queries
-        pack_ref[0, start:, :] = extra.astype(BF16)
-
-    @pl.when(step < heads)
+        hash_heads()
+
+    @pl.when(jnp.logical_and(step > 0, step < steps))
     def _():
-        finish_head()
-        hashed_ref[...] = hash_head()
-
-    @pl.when(step == heads)
+        finish_heads()
+        hash_heads()
+
+    @pl.when(step == steps)
     def _():
-        finish_head()
+        finish_heads()
 
 
 def build_sketches(head_out, grad_out, codes, mask, query_ids):
@@ -102,31 +106,33 @@
     queries = query_ids.shape[0]
     rows = 2 * WIDTH + 2 * queries + EXTRA
     last = lambda h: jnp.maximum(h - 1, 0)
+    small = [codes, mask[None, :], query_ids[None, :]]
+    small = [pltpu.with_memory_space_constraint(x, pltpu.HBM) for x in small]
     return pl.pallas_call(
         functools.partial(sketch_kernel, math.sqrt(WIDTH / width)),
-        grid=(heads + 1,),
+        grid=(heads // GROUP + 1,),
         in_specs=[
             pl.BlockSpec((heads, width), lambda h: (0, 0)),
             pl.BlockSpec((tokens, width), lambda h: (0, 0)),
-            pl.BlockSpec((tokens, WIDTH), lambda h: (0, last(h))),
+            pl.BlockSpec((tokens, GROUP * WIDTH), lambda h: (0, last(h))),
             pl.BlockSpec((1, tokens), lambda h: (0, 0)),
             pl.BlockSpec((1, queries), lambda h: (0, 0)),
         ],
         out_specs=[
-            pl.BlockSpec((tokens, WIDTH), lambda h: (0, last(h))),
-            pl.BlockSpec((1, rows, HALF), lambda h: (last(h), 0, 0)),
+            pl.BlockSpec((tokens, GROUP * WIDTH), lambda h: (0, last(h))),
+            pl.BlockSpec((GROUP, rows, HALF), lambda h: (last(h), 0, 0)),
         ],
         out_shape=[
             jax.ShapeDtypeStruct((tokens, heads * WIDTH), BF16),
-            jax.ShapeDtypeStruct((heads, rows, HALF), BF16),
+            pltpu.HBM((heads, rows, HALF), BF16),
         ],
         scratch_shapes=[
-            pltpu.VMEM((tokens, WIDTH), F32),
+            pltpu.VMEM((tokens, GROUP * WIDTH), F32),
             pltpu.VMEM((queries, tokens), BF16),
         ],
         compiler_params=params(),
         name="sketch",
-    )(codes, grad_out, head_out, mask[None, :], query_ids[None, :])
+    )(small[0], grad_out, head_out, small[1], small[2])
 
 
 def solve_kernel(pack_ref, solved_ref, count_ref, work_ref, answer_ref):

time: 158 us -> 155 us (0.981)
  Pallas kernels: 69.4 us -> 66.2 us
    pallas_call x1, Pallas kernels: 24.3 us -> 21.1 us  [build_sketches(): pl.pallas_call(functools.partial(sketch_kernel, math.sqrt(WIDTH / width))...]
where the time goes in v3:
time: 155 us; the launch traced here: 154 us
  blocking collectives  75.6 us (49%)
  Pallas kernels  66.2 us (43%)
  waiting for transfers between devices  5.25 us (3%)
  starting transfers between devices  4.3 us (3%)
  local copies, waits for them, and re-layouts  2.16 us (1%)
    all_to_all x4, blocking collectives, exchange(): return lax.all_to_all(array, axis, split_axis=0, concat_axis=0, tiled=True)  75.6 us
    pallas_call x1, Pallas kernels, solve(): pl.pallas_call(solve_kernel, out_shape=[jax.ShapeDtypeStruct((sources, qu...  42.2 us
    pallas_call x1, Pallas kernels, build_sketches(): pl.pallas_call(functools.partial(sketch_kernel, math.sqrt(WIDTH / width))...  21.1 us
    all_to_all x1, waiting for transfers between devices, exchange(): return lax.all_to_all(array, axis, split_axis=0, concat_axis=0, tiled=True)  5.25 us
    all_to_all x1, starting transfers between devices, exchange(): return lax.all_to_all(array, axis, split_axis=0, concat_axis=0, tiled=True)  4.3 us
  transfers between devices with their start and end apart: 1, of which 1 were waited for; matrix products, arithmetic and copies ran while one was open for 1% of the time, Pallas kernels for 0%

profile of v3, /device:TPU:0, one launch (start us, length us, event | category | flops | bytes accessed | tf_op | source)
XLA Modules:
  0.0 154.2 jit_solution(389028287364027457)
XLA Ops:
  0.0 0.0 copy-start.1
  0.0 2.0 %copy-done.1 = bf16[1,512,3584]{2,1,0:T(8,128)(2,1)S(1)} copy-done((bf16[1,512,3584]{2,1,0:T(8,128)(2,1)S(1)}, bf16[1,512,3584]{2,1,0:T(8,128)(2,1)}, u32[]{:S(2)}) %copy-start.1) | copy-done | bytes 3670040
  2.0 21.1 %sketch.1 = (bf16[512,4096]{1,0:T(8,128)(2,1)}, bf16[16,656,128]{2,1,0:T(8,128)(2,1)}) custom-call(s32[16,3584]{1,0:T(8,128)} %bitcast.12, bf16[512,3584]{1,0:T(8,128)(2,1)S(1)} %bitcast.9, bf16[512,4096]{1,0:T(8,128)(2,1)} %bitcast.11, s32[1,512]{1,0:T(1,128)} %bitcast.14, s32[1,64]{1,0:T(1,128)} %bitcast.15), custom_call_target="tpu_custom_call" | custom-call | tf_op jit(solution)/shard_map/sketch/pallas_call | solution.py:111
  23.1 0.0 copy-start
  23.1 43.5 %all_to_all.25.pack_ref = bf16[16,656,128]{2,1,0:T(8,128)(2,1)S(1)} all-to-all(bf16[16,656,128]{2,1,0:T(8,128)(2,1)} %get-tuple-element.12), channel_id=1, replica_groups=mesh['seq_0'=4,'seq_1'=4,'rep_0'=4,'rep_1'=2] {'seq_0','seq_1'}, dimensions={0} | all-to-all | bytes 5373952 | tf_op jit(solution)/shard_map/all_to_all | solution.py:310
  66.6 42.2 %solve.1 = (bf16[16,64,256]{2,1,0:T(8,128)(2,1)S(1)}, f32[8,128]{1,0:T(8,128)S(1)}) custom-call(bf16[16,656,128]{2,1,0:T(8,128)(2,1)S(1)} %all_to_all.25.pack_ref), custom_call_target="tpu_custom_call" | custom-call | tf_op jit(solution)/shard_map/solve/pallas_call | solution.py:224
  108.8 13.6 %all_to_all.26.solved_ref = bf16[16,64,256]{2,1,0:T(8,128)(2,1)S(1)} all-to-all(bf16[16,64,256]{2,1,0:T(8,128)(2,1)S(1)} %get-tuple-element.13), channel_id=1, replica_groups=mesh['seq_0'=4,'seq_1'=4,'rep_0'=4,'rep_1'=2] {'seq_0','seq_1'}, dimensions={0} | all-to-all | bytes 1048576 | tf_op jit(solution)/shard_map/all_to_all | solution.py:310
  122.4 0.0 copy-done
  122.4 1.9 %score.1 = f32[8,32,128]{2,1,0:T(8,128)} custom-call(bf16[512,4096]{1,0:T(8,128)(2,1)S(1)} %copy-done, bf16[16,64,256]{2,1,0:T(8,128)(2,1)S(1)} %all_to_all.26.solved_ref), custom_call_target="tpu_custom_call" | custom-call | tf_op jit(solution)/shard_map/score/pallas_call | solution.py:255
  124.4 4.3 %all-to-all-start.2 = ((f32[8,32,128]{2,1,0:T(8,128)}), f32[8,32,128]{2,1,0:T(8,128)S(1)}, u32[]{:S(2)}, u32[]{:S(2)}) async-start(f32[8,32,128]{2,1,0:T(8,128)} %score.1), calls=%async_computation.2 | async-start | bytes 262144 | tf_op jit(solution)/shard_map/all_to_all | solution.py:310
  128.7 0.8 convert_bitcast_fusion
  129.4 0.1 copy.8.mask_ref
  129.5 5.2 %all-to-all-done.2.part_ref = f32[8,32,128]{2,1,0:T(8,128)S(1)} async-done(((f32[8,32,128]{2,1,0:T(8,128)}), f32[8,32,128]{2,1,0:T(8,128)S(1)}, u32[]{:S(2)}, u32[]{:S(2)}) %all-to-all-start.2) | async-done | bytes 131104 | tf_op jit(solution)/shard_map/all_to_all | solution.py:310
  134.8 0.2 squares.1
  135.0 7.6 %all_to_all.27 = f32[8,1,128]{2,1,0:T(1,128)S(1)} all-to-all(f32[8,1,128]{2,1,0:T(1,128)S(1)} %broadcast_in_dim.18), channel_id=1, replica_groups=mesh['seq_0'=4,'seq_1'=4,'rep_0'=4,'rep_1'=2] {'rep_0','rep_1'}, dimensions={0} | all-to-all | bytes 8192 | tf_op jit(solution)/shard_map/all_to_all | solution.py:310
  142.7 10.8 %all_to_all.28.square_ref = f32[16,1,128]{2,1,0:T(1,128)S(1)} all-to-all(f32[16,1,128]{2,1,0:T(1,128)S(1)} %broadcast_in_dim.19), channel_id=1, replica_groups=mesh['seq_0'=4,'seq_1'=4,'rep_0'=4,'rep_1'=2] {'seq_0','seq_1'}, dimensions={0} | all-to-all | bytes 16384 | tf_op jit(solution)/shard_map/all_to_all | solution.py:310
  153.5 0.7 finish.1
  (3 shorter events, 0.0 us)
Async XLA Ops:
  0.0 2.0 %copy-start.1 = (bf16[1,512,3584]{2,1,0:T(8,128)(2,1)S(1)}, bf16[1,512,3584]{2,1,0:T(8,128)(2,1)}, u32[]{:S(2)}) copy-start(bf16[1,512,3584]{2,1,0:T(8,128)(2,1)} %param.6) | copy-start | bytes 11010052
  23.1 99.3 %copy-start = (bf16[512,4096]{1,0:T(8,128)(2,1)S(1)}, bf16[512,4096]{1,0:T(8,128)(2,1)}, u32[]{:S(2)}) copy-start(bf16[512,4096]{1,0:T(8,128)(2,1)} %get-tuple-element.11.sketch_ref) | copy-start | bytes 12582916
  124.4 10.4 %all-to-all-start.2 = ((f32[8,32,128]{2,1,0:T(8,128)}), f32[8,32,128]{2,1,0:T(8,128)S(1)}, u32[]{:S(2)}, u32[]{:S(2)}) async-start(f32[8,32,128]{2,1,0:T(8,128)} %score.1), calls=%async_computation.2 | async-start | bytes 262144 | tf_op jit(solution)/shard_map/all_to_all | solution.py:310

commit v4 on v3

--- a/solution.py
+++ b/solution.py
@@ -20,6 +20,7 @@
 EXTRA = 16
 TURNS = 12
 GROUP = 4
+SLOTS = 16
 F32 = jnp.float32
 BF16 = jnp.bfloat16
 
@@ -33,8 +34,17 @@
     return pltpu.CompilerParams(vmem_limit_bytes=mib * 2**20)
 
 
+def places(query_ids, tokens):
+    shape = (query_ids.shape[1], query_ids.shape[1])
+    sub, lane = lax.broadcasted_iota(jnp.int32, shape, 0), lax.broadcasted_iota(jnp.int32, shape, 1)
+    across = jnp.broadcast_to(lax.div(query_ids, jnp.int32(tokens)).astype(F32), shape)
+    source = jnp.sum(jnp.where(sub == lane, across, 0.0), 1, keepdims=True)
+    earlier = jnp.logical_and(across == source, lane < sub)
+    return source, jnp.sum(jnp.where(earlier, 1.0, 0.0), 1, keepdims=True)
+
+
 def sketch_kernel(scale, code_ref, grad_ref, out_ref, mask_ref, query_ref, sketch_ref, pack_ref,
-                  hashed_ref, picks_ref):
+                  chosen_ref, crowded_ref, hashed_ref, picks_ref):
     tokens, width = grad_ref.shape
     queries = query_ref.shape[1]
     group = pack_ref.shape[0]
@@ -76,18 +86,32 @@
                 pack_ref[g, start : start + HALF, :] = top
                 start += WIDTH
                 pack_ref[g, start : start + HALF, :] = (value - top.astype(F32)).astype(BF16)
+            chosen_ref[g, :queries, :] = chosen[:queries, :HALF]
+            chosen_ref[g, queries:, :] = chosen[:queries, HALF:]
             start = 2 * WIDTH
-            pack_ref[g, start : start + queries, :] = chosen[:, :HALF]
-            start += queries
-            pack_ref[g, start : start + queries, :] = chosen[:, HALF:]
-            start += queries
+            pack_ref[g, start : start + SLOTS, :] = chosen[queries:, :HALF]
+            start += SLOTS
+            pack_ref[g, start : start + SLOTS, :] = chosen[queries:, HALF:]
+            start += SLOTS
             pack_ref[g, start:, :] = extra.astype(BF16)
 
     @pl.when(step == 0)
     def _():
         local = query_ref[...] - lax.axis_index(SEQ) * tokens
         token = lax.broadcasted_iota(jnp.int32, (tokens, queries), 0)
-        picks_ref[...] = jnp.where(token == local, 1.0, 0.0).T.astype(BF16)
+        picks = jnp.where(token == local, 1.0, 0.0).T.astype(BF16)
+        own = jnp.logical_and(local >= 0, local < tokens)
+        before = lax.broadcasted_iota(jnp.int32, (queries, queries), 0)
+        before = before < lax.broadcasted_iota(jnp.int32, (queries, queries), 1)
+        before = jnp.where(before, 1.0, 0.0).astype(BF16)
+        ones = jnp.broadcast_to(jnp.where(own, 1.0, 0.0), (SLOTS, queries))
+        rank = dot(ones.astype(BF16), before, 1, 0)
+        slot = lax.broadcasted_iota(jnp.int32, (SLOTS, queries), 0).astype(F32)
+        slots = jnp.where(rank == slot, ones, 0.0).astype(BF16)
+        picks_ref[:queries, :] = picks
+        picks_ref[queries:, :] = dot(slots, picks, 1, 0).astype(BF16)
+        _, rank = places(query_ref[...], tokens)
+        crowded_ref[0, 0] = (jnp.max(rank) >= SLOTS).astype(jnp.int32)
         hash_heads()
 
     @pl.when(jnp.logical_and(step > 0, step < steps))
@@ -104,10 +128,10 @@
     heads, width = codes.shape
     tokens = grad_out.shape[0]
     queries = query_ids.shape[0]
-    rows = 2 * WIDTH + 2 * queries + EXTRA
+    rows = 2 * WIDTH + 2 * SLOTS + EXTRA
     last = lambda h: jnp.maximum(h - 1, 0)
-    small = [codes, mask[None, :], query_ids[None, :]]
-    small = [pltpu.with_memory_space_constraint(x, pltpu.HBM) for x in small]
+    held = [codes, mask[None, :], query_ids[None, :], grad_out, head_out]
+    held = [pltpu.with_memory_space_constraint(x, pltpu.HBM) for x in held]
     return pl.pallas_call(
         functools.partial(sketch_kernel, math.sqrt(WIDTH / width)),
         grid=(heads // GROUP + 1,),
@@ -121,23 +145,27 @@
         out_specs=[
             pl.BlockSpec((tokens, GROUP * WIDTH), lambda h: (0, last(h))),
             pl.BlockSpec((GROUP, rows, HALF), lambda h: (last(h), 0, 0)),
+            pl.BlockSpec((GROUP, 2 * queries, HALF), lambda h: (last(h), 0, 0)),
+            pl.BlockSpec(memory_space=pltpu.SMEM),
         ],
         out_shape=[
-            jax.ShapeDtypeStruct((tokens, heads * WIDTH), BF16),
+            pltpu.HBM((tokens, heads * WIDTH), BF16),
             pltpu.HBM((heads, rows, HALF), BF16),
+            pltpu.HBM((heads, 2 * queries, HALF), BF16),
+            jax.ShapeDtypeStruct((1, 1), jnp.int32),
         ],
         scratch_shapes=[
             pltpu.VMEM((tokens, GROUP * WIDTH), F32),
-            pltpu.VMEM((queries, tokens), BF16),
+            pltpu.VMEM((queries + SLOTS, tokens), BF16),
         ],
         compiler_params=params(),
         name="sketch",
-    )(small[0], grad_out, head_out, small[1], small[2])
-
-
-def solve_kernel(pack_ref, solved_ref, count_ref, work_ref, answer_ref):
+    )(held[0], held[3], held[4], held[1], held[2])
+
+
+def solve_kernel(tokens, pack_ref, query_ref, spare_ref, solved_ref, count_ref, work_ref, answer_ref):
     sources = pack_ref.shape[0]
-    queries = (pack_ref.shape[1] - 2 * WIDTH - EXTRA) // 2
+    queries = query_ref.shape[1]
 
     def add(start, rows):
         total = pack_ref[0, start : start + rows, :].astype(F32)
@@ -147,9 +175,19 @@
 
     side = add(0, HALF) + add(WIDTH, HALF)
     both = add(HALF, HALF) + add(WIDTH + HALF, HALF)
-    left = add(2 * WIDTH, queries)
-    right = add(2 * WIDTH + queries, queries)
-    extra = add(2 * WIDTH + 2 * queries, EXTRA)
+    extra = add(2 * WIDTH + 2 * SLOTS, EXTRA)
+
+    source, rank = places(query_ref[...], tokens)
+    place = lax.broadcasted_iota(jnp.int32, (queries, sources * SLOTS), 1).astype(F32)
+    picks = jnp.where(place == source * SLOTS + rank, 1.0, 0.0).astype(BF16)
+
+    def picked(start):
+        rows = [pack_ref[s, start : start + SLOTS, :] for s in range(sources)]
+        return dot(picks, jnp.concatenate(rows, 0), 1, 0)
+
+    crowded = jnp.max(rank) >= SLOTS
+    left = jnp.where(crowded, spare_ref[:, :HALF], picked(2 * WIDTH))
+    right = jnp.where(crowded, spare_ref[:, HALF:], picked(2 * WIDTH + SLOTS))
     extra = extra[0:2, :] + extra[2:4, :]
     count = extra[1:2, :] + 1.0
     count_ref[...] = jnp.broadcast_to(count, count_ref.shape)
@@ -218,11 +256,11 @@
         solved_ref[s] = solved
 
 
-def solve(packs):
-    sources, rows, _ = packs.shape
-    queries = (rows - 2 * WIDTH - EXTRA) // 2
-    return pl.pallas_call(
-        solve_kernel,
+def solve(packs, query_ids, spare, tokens):
+    sources = packs.shape[0]
+    queries = query_ids.shape[0]
+    return pl.pallas_call(
+        functools.partial(solve_kernel, tokens),
         out_shape=[
             jax.ShapeDtypeStruct((sources, queries, WIDTH), BF16),
             jax.ShapeDtypeStruct((8, HALF), F32),
@@ -233,16 +271,27 @@
         ],
         compiler_params=params(),
         name="solve",
-    )(packs)
+    )(packs, query_ids[None, :], spare)
+
+
+def spare_rows(chosen, crowded):
+    queries = chosen.shape[1] // 2
+
+    def exchanged(rows):
+        total = exchange(rows, SEQ).astype(F32).sum(0)
+        return jnp.concatenate([total[:queries], total[queries:]], 1)
+
+    def nothing(rows):
+        return jnp.zeros((queries, WIDTH), F32)
+
+    return lax.cond(crowded[0, 0] > 0, exchanged, nothing, chosen)
 
 
 def score_kernel(sketch_ref, solved_ref, part_ref):
     heads, queries, _ = solved_ref.shape
     owners = part_ref.shape[0]
-    total = None
-    for h in range(heads):
-        part = dot(sketch_ref[:, h * WIDTH : (h + 1) * WIDTH], solved_ref[h], 1, 1)
-        total = part if total is None else total + part
+    solved = jnp.concatenate([solved_ref[h] for h in range(heads)], 1)
+    total = dot(sketch_ref[...], solved, 1, 1)
     size = total.shape[0] // owners
     for o in range(owners):
         block = total[o * size : (o + 1) * size]
@@ -320,8 +369,11 @@
     size = tokens // owners
     own_mask = lax.dynamic_slice_in_dim(loss_mask, lax.axis_index(REP) * size, size, 0)
     own_mask = own_mask.astype(F32)[:, None]
-    sketch, packs = build_sketches(head_out[0], grad_out[0], hash_codes[0], loss_mask, query_ids)
-    solved, count = solve(exchange(packs, SEQ))
+    sketch, packs, chosen, crowded = build_sketches(
+        head_out[0], grad_out[0], hash_codes[0], loss_mask, query_ids
+    )
+    spare = spare_rows(chosen, crowded)
+    solved, count = solve(exchange(packs, SEQ), query_ids, spare, tokens)
     parts = score(sketch, exchange(solved, SEQ), owners)
     contrib, square = squares(exchange(parts, REP), own_mask)
     square = from_everyone(square, REP).sum(0)

time: 155 us -> 151 us (0.974)
  blocking collectives: 75.6 us -> 71.3 us
  local copies, waits for them, and re-layouts: 2.16 us -> 0.13 us
    all_to_all x4, blocking collectives: 75.6 us -> 71.3 us  [exchange(): return lax.all_to_all(array, axis, split_axis=0, concat_axis=0, tiled=True)]
    unnamed x4, local copies, waits for them, and re-layouts: 2.04 us -> 0.01 us
where the time goes in v4:
time: 151 us; the launch traced here: 150 us
  blocking collectives  71.3 us (47%)
  Pallas kernels  67.6 us (45%)
  waiting for transfers between devices  5.25 us (3%)
  starting transfers between devices  4.31 us (3%)
    all_to_all x4, blocking collectives, exchange(): return lax.all_to_all(array, axis, split_axis=0, concat_axis=0, tiled=True)  71.3 us
    pallas_call x1, Pallas kernels, solve(): pl.pallas_call(functools.partial(solve_kernel, tokens), out_shape=[jax.Sh...  42.4 us
    pallas_call x1, Pallas kernels, build_sketches(): pl.pallas_call(functools.partial(sketch_kernel, math.sqrt(WIDTH / width))...  22.3 us
    all_to_all x1, waiting for transfers between devices, exchange(): return lax.all_to_all(array, axis, split_axis=0, concat_axis=0, tiled=True)  5.25 us
    all_to_all x1, starting transfers between devices, exchange(): return lax.all_to_all(array, axis, split_axis=0, concat_axis=0, tiled=True)  4.31 us
  transfers between devices with their start and end apart: 1, of which 1 were waited for; matrix products, arithmetic and copies ran while one was open for 1% of the time, Pallas kernels for 0%

profile of v4, /device:TPU:0, one launch (start us, length us, event | category | flops | bytes accessed | tf_op | source)
XLA Modules:
  0.0 150.1 jit_solution(705526507372023159)
XLA Ops:
  0.0 22.3 %sketch.1 = (bf16[512,4096]{1,0:T(8,128)(2,1)}, bf16[16,560,128]{2,1,0:T(8,128)(2,1)}, bf16[16,128,128]{2,1,0:T(8,128)(2,1)}, s32[1,1]{1,0:T(1,128)}) custom-call(s32[16,3584]{1,0:T(8,128)} %bitcast.15, bf16[512,3584]{1,0:T(8,128)(2,1)} %bitcast.14, bf16[512,4096]{1,0:T(8,128)(2,1)} %bitcast.13, s32[1,512]{1,0:T(1,128)} %bitcast.17, s32[1,64]{1,0:T(1,128)} %bitcast.10), custom_call_target="tpu_custom_call" | custom-call | tf_op jit(solution)/shard_map/sketch/pallas_call | solution.py:135
  22.3 0.0 copy-start.1
  23.0 0.0 copy-start
  23.0 38.9 %all_to_all.30.pack_ref = bf16[16,560,128]{2,1,0:T(8,128)(2,1)S(1)} all-to-all(bf16[16,560,128]{2,1,0:T(8,128)(2,1)} %get-tuple-element.18), channel_id=1, replica_groups=mesh['seq_0'=4,'seq_1'=4,'rep_0'=4,'rep_1'=2] {'seq_0','seq_1'}, dimensions={0} | all-to-all | bytes 4587520 | tf_op jit(solution)/shard_map/all_to_all | solution.py:359
  61.9 0.0 copy-done.1
  61.9 42.4 %solve.1 = (bf16[16,64,256]{2,1,0:T(8,128)(2,1)S(1)}, f32[8,128]{1,0:T(8,128)S(1)}) custom-call(bf16[16,560,128]{2,1,0:T(8,128)(2,1)S(1)} %all_to_all.30.pack_ref, s32[1,64]{1,0:T(1,128)S(1)} %bitcast.11, f32[64,256]{1,0:T(8,128)S(1)} %get-tuple-element.27.spare_ref), custom_call_target="tpu_custom_call" | custom-call | tf_op jit(solution)/shard_map/solve/pallas_call | solution.py:262
  104.4 13.9 %all_to_all.31.solved_ref = bf16[16,64,256]{2,1,0:T(8,128)(2,1)S(1)} all-to-all(bf16[16,64,256]{2,1,0:T(8,128)(2,1)S(1)} %get-tuple-element.21), channel_id=1, replica_groups=mesh['seq_0'=4,'seq_1'=4,'rep_0'=4,'rep_1'=2] {'seq_0','seq_1'}, dimensions={0} | all-to-all | bytes 1048576 | tf_op jit(solution)/shard_map/all_to_all | solution.py:359
  118.3 0.0 copy-done
  118.3 1.9 %score.1 = f32[8,32,128]{2,1,0:T(8,128)} custom-call(bf16[512,4096]{1,0:T(8,128)(2,1)S(1)} %copy-done, bf16[16,64,256]{2,1,0:T(8,128)(2,1)S(1)} %all_to_all.31.solved_ref), custom_call_target="tpu_custom_call" | custom-call | tf_op jit(solution)/shard_map/score/pallas_call | solution.py:304
  120.2 4.3 %all-to-all-start.3 = ((f32[8,32,128]{2,1,0:T(8,128)}), f32[8,32,128]{2,1,0:T(8,128)S(1)}, u32[]{:S(2)}, u32[]{:S(2)}) async-start(f32[8,32,128]{2,1,0:T(8,128)} %score.1), calls=%async_computation.3 | async-start | bytes 262144 | tf_op jit(solution)/shard_map/all_to_all | solution.py:359
  124.5 0.8 convert_bitcast_fusion
  125.3 0.1 copy.8.mask_ref
  125.4 5.2 %all-to-all-done.3.part_ref = f32[8,32,128]{2,1,0:T(8,128)S(1)} async-done(((f32[8,32,128]{2,1,0:T(8,128)}), f32[8,32,128]{2,1,0:T(8,128)S(1)}, u32[]{:S(2)}, u32[]{:S(2)}) %all-to-all-start.3) | async-done | bytes 131104 | tf_op jit(solution)/shard_map/all_to_all | solution.py:359
  130.7 0.2 squares.1
  130.9 7.6 %all_to_all.32 = f32[8,1,128]{2,1,0:T(1,128)S(1)} all-to-all(f32[8,1,128]{2,1,0:T(1,128)S(1)} %broadcast_in_dim.19), channel_id=1, replica_groups=mesh['seq_0'=4,'seq_1'=4,'rep_0'=4,'rep_1'=2] {'rep_0','rep_1'}, dimensions={0} | all-to-all | bytes 8192 | tf_op jit(solution)/shard_map/all_to_all | solution.py:359
  138.5 10.8 %all_to_all.33.square_ref = f32[16,1,128]{2,1,0:T(1,128)S(1)} all-to-all(f32[16,1,128]{2,1,0:T(1,128)S(1)} %broadcast_in_dim.20), channel_id=1, replica_groups=mesh['seq_0'=4,'seq_1'=4,'rep_0'=4,'rep_1'=2] {'seq_0','seq_1'}, dimensions={0} | all-to-all | bytes 16384 | tf_op jit(solution)/shard_map/all_to_all | solution.py:359
  149.4 0.7 finish.1
  (5 shorter events, 0.1 us)
Async XLA Ops:
  22.3 39.6 %copy-start.1 = (s32[64]{0:T(128)S(1)}, s32[64]{0:T(128)}, u32[]{:S(2)}) copy-start(s32[64]{0:T(128)} %param.11) | copy-start | bytes 772
  23.0 95.3 %copy-start = (bf16[512,4096]{1,0:T(8,128)(2,1)S(1)}, bf16[512,4096]{1,0:T(8,128)(2,1)}, u32[]{:S(2)}) copy-start(bf16[512,4096]{1,0:T(8,128)(2,1)} %get-tuple-element.17.sketch_ref) | copy-start | bytes 12582916
  120.2 10.4 %all-to-all-start.3 = ((f32[8,32,128]{2,1,0:T(8,128)}), f32[8,32,128]{2,1,0:T(8,128)S(1)}, u32[]{:S(2)}, u32[]{:S(2)}) async-start(f32[8,32,128]{2,1,0:T(8,128)} %score.1), calls=%async_computation.3 | async-start | bytes 262144 | tf_op jit(solution)/shard_map/all_to_all | solution.py:359

commit v5 on v4

--- a/solution.py
+++ b/solution.py
@@ -17,7 +17,7 @@
 FLOOR = 1e-06
 WIDTH = 256
 HALF = 128
-EXTRA = 16
+EXTRA = 8
 TURNS = 12
 GROUP = 4
 SLOTS = 16
@@ -316,7 +316,11 @@
         total = total + part_ref[o]
     contrib_ref[...] = total
     rows, queries = total.shape[0], total.shape[1] // 2
-    mask = mask_ref[...]
+    positions = mask_ref.shape[1]
+    shape = (positions // owners, positions)
+    first = lax.axis_index(REP) * shape[0]
+    own = lax.broadcasted_iota(jnp.int32, shape, 1) == lax.broadcasted_iota(jnp.int32, shape, 0) + first
+    mask = jnp.sum(jnp.where(own, mask_ref[...].astype(F32), 0.0), 1, keepdims=True)
     top = jnp.sum(mask[:rows] * total * total, 0, keepdims=True)
     end = jnp.sum(mask[rows:] * total * total, 0, keepdims=True)
     square = top[:, :queries] + end[:, queries:]
@@ -333,7 +337,7 @@
         ],
         compiler_params=params(),
         name="squares",
-    )(parts, mask)
+    )(parts, mask[None, :])
 
 
 def finish_kernel(contrib_ref, square_ref, count_ref, result_ref):
@@ -366,16 +370,13 @@
 def on_device(head_out, grad_out, hash_codes, loss_mask, query_ids):
     tokens = loss_mask.shape[0]
     owners = lax.axis_size(REP)
-    size = tokens // owners
-    own_mask = lax.dynamic_slice_in_dim(loss_mask, lax.axis_index(REP) * size, size, 0)
-    own_mask = own_mask.astype(F32)[:, None]
     sketch, packs, chosen, crowded = build_sketches(
         head_out[0], grad_out[0], hash_codes[0], loss_mask, query_ids
     )
     spare = spare_rows(chosen, crowded)
     solved, count = solve(exchange(packs, SEQ), query_ids, spare, tokens)
     parts = score(sketch, exchange(solved, SEQ), owners)
-    contrib, square = squares(exchange(parts, REP), own_mask)
+    contrib, square = squares(exchange(parts, REP), loss_mask)
     square = from_everyone(square, REP).sum(0)
     return finish(contrib, from_everyone(square, SEQ), count)
 

time: 151 us -> 149 us (0.987)
  blocking collectives: 71.3 us -> 81.1 us
  waiting for transfers between devices: 5.25 us -> 0 us
  starting transfers between devices: 4.31 us -> 0 us
    all_to_all x4 -> x5, blocking collectives: 71.3 us -> 81.1 us  [exchange(): return lax.all_to_all(array, axis, split_axis=0, concat_axis=0, tiled=True)]
    all_to_all x1 -> x0, waiting for transfers between devices: 5.25 us -> none  [exchange(): return lax.all_to_all(array, axis, split_axis=0, concat_axis=0, tiled=True)]
    all_to_all x1 -> x0, starting transfers between devices: 4.31 us -> none  [exchange(): return lax.all_to_all(array, axis, split_axis=0, concat_axis=0, tiled=True)]
  transfers between devices with their start and end apart: 1 -> 0, of which waited for: 1 -> 0; matrix products, arithmetic and copies ran while one was open for 1% -> 0% of each run, Pallas kernels for 0% -> 0%
where the time goes in v5:
time: 149 us
  blocking collectives  81.1 us (54%)
  Pallas kernels  67.1 us (45%)
    all_to_all x5, blocking collectives, exchange(): return lax.all_to_all(array, axis, split_axis=0, concat_axis=0, tiled=True)  81.1 us
    pallas_call x1, Pallas kernels, solve(): pl.pallas_call(functools.partial(solve_kernel, tokens), out_shape=[jax.Sh...  42.4 us
    pallas_call x1, Pallas kernels, build_sketches(): pl.pallas_call(functools.partial(sketch_kernel, math.sqrt(WIDTH / width))...  22.4 us

profile of v5, /device:TPU:0, one launch (start us, length us, event | category | flops | bytes accessed | tf_op | source)
XLA Modules:
  0.0 149.0 jit_solution(4348023317463129725)
XLA Ops:
  0.0 22.4 %sketch.1 = (bf16[512,4096]{1,0:T(8,128)(2,1)}, bf16[16,552,128]{2,1,0:T(8,128)(2,1)}, bf16[16,128,128]{2,1,0:T(8,128)(2,1)}, s32[1,1]{1,0:T(1,128)}) custom-call(s32[16,3584]{1,0:T(8,128)} %bitcast.15, bf16[512,3584]{1,0:T(8,128)(2,1)} %bitcast.14, bf16[512,4096]{1,0:T(8,128)(2,1)} %bitcast.13, s32[1,512]{1,0:T(1,128)} %bitcast.8, s32[1,64]{1,0:T(1,128)} %bitcast.10), custom_call_target="tpu_custom_call" | custom-call | tf_op jit(solution)/shard_map/sketch/pallas_call | solution.py:135
  22.4 0.0 copy-start.2
  23.1 0.0 copy-start
  23.1 38.6 %all_to_all.30.pack_ref = bf16[16,552,128]{2,1,0:T(8,128)(2,1)S(1)} all-to-all(bf16[16,552,128]{2,1,0:T(8,128)(2,1)} %get-tuple-element.18), channel_id=1, replica_groups=mesh['seq_0'=4,'seq_1'=4,'rep_0'=4,'rep_1'=2] {'seq_0','seq_1'}, dimensions={0} | all-to-all | bytes 4521984 | tf_op jit(solution)/shard_map/all_to_all | solution.py:363
  61.7 0.0 copy-done.2
  61.7 0.0 copy-start.1
  61.7 42.4 %solve.1 = (bf16[16,64,256]{2,1,0:T(8,128)(2,1)S(1)}, f32[8,128]{1,0:T(8,128)S(1)}) custom-call(bf16[16,552,128]{2,1,0:T(8,128)(2,1)S(1)} %all_to_all.30.pack_ref, s32[1,64]{1,0:T(1,128)S(1)} %bitcast.11, f32[64,256]{1,0:T(8,128)S(1)} %get-tuple-element.27.spare_ref), custom_call_target="tpu_custom_call" | custom-call | tf_op jit(solution)/shard_map/solve/pallas_call | solution.py:262
  104.1 13.9 %all_to_all.31.solved_ref = bf16[16,64,256]{2,1,0:T(8,128)(2,1)S(1)} all-to-all(bf16[16,64,256]{2,1,0:T(8,128)(2,1)S(1)} %get-tuple-element.21), channel_id=1, replica_groups=mesh['seq_0'=4,'seq_1'=4,'rep_0'=4,'rep_1'=2] {'seq_0','seq_1'}, dimensions={0} | all-to-all | bytes 1048576 | tf_op jit(solution)/shard_map/all_to_all | solution.py:363
  118.0 0.0 copy-done
  118.0 1.3 score.1
  119.3 10.2 %all_to_all.32.part_ref = f32[8,32,128]{2,1,0:T(8,128)S(1)} all-to-all(f32[8,32,128]{2,1,0:T(8,128)S(1)} %score.1), channel_id=1, replica_groups=mesh['seq_0'=4,'seq_1'=4,'rep_0'=4,'rep_1'=2] {'rep_0','rep_1'}, dimensions={0} | all-to-all | bytes 262144 | tf_op jit(solution)/shard_map/all_to_all | solution.py:363
  129.5 0.0 copy-done.1
  129.5 0.2 squares.1
  129.8 7.6 %all_to_all.33 = f32[8,1,128]{2,1,0:T(1,128)S(1)} all-to-all(f32[8,1,128]{2,1,0:T(1,128)S(1)} %broadcast_in_dim.16), channel_id=1, replica_groups=mesh['seq_0'=4,'seq_1'=4,'rep_0'=4,'rep_1'=2] {'rep_0','rep_1'}, dimensions={0} | all-to-all | bytes 8192 | tf_op jit(solution)/shard_map/all_to_all | solution.py:363
  137.4 10.8 %all_to_all.34.square_ref = f32[16,1,128]{2,1,0:T(1,128)S(1)} all-to-all(f32[16,1,128]{2,1,0:T(1,128)S(1)} %broadcast_in_dim.17), channel_id=1, replica_groups=mesh['seq_0'=4,'seq_1'=4,'rep_0'=4,'rep_1'=2] {'seq_0','seq_1'}, dimensions={0} | all-to-all | bytes 16384 | tf_op jit(solution)/shard_map/all_to_all | solution.py:363
  148.3 0.7 finish.1
  (5 shorter events, 0.1 us)
Async XLA Ops:
  22.4 39.3 %copy-start.2 = (s32[64]{0:T(128)S(1)}, s32[64]{0:T(128)}, u32[]{:S(2)}) copy-start(s32[64]{0:T(128)} %param.11) | copy-start | bytes 772
  23.1 94.9 %copy-start = (bf16[512,4096]{1,0:T(8,128)(2,1)S(1)}, bf16[512,4096]{1,0:T(8,128)(2,1)}, u32[]{:S(2)}) copy-start(bf16[512,4096]{1,0:T(8,128)(2,1)} %get-tuple-element.17.sketch_ref) | copy-start | bytes 12582916
  61.7 67.8 %copy-start.1 = (s32[512]{0:T(512)S(1)}, s32[512]{0:T(512)}, u32[]{:S(2)}) copy-start(s32[512]{0:T(512)} %param.10) | copy-start | bytes 6148

commit v6 on v5

--- a/solution.py
+++ b/solution.py
@@ -70,8 +70,9 @@
             columns = slice(g * WIDTH, (g + 1) * WIDTH)
             sketch = (out_ref[:, columns].astype(F32) * hashed_ref[:, columns] * scale).astype(BF16)
             sketch_ref[:, columns] = sketch
-            gram = dot(sketch.T * mask, sketch, 1, 0)
-            chosen = dot(picks_ref[...], sketch, 1, 0).astype(BF16)
+            sides = jnp.concatenate([sketch.T * mask, picks_ref[...]], 0)
+            products = dot(sides, sketch, 1, 0)
+            gram, chosen = products[:WIDTH], products[WIDTH:].astype(BF16)
 
             upper, lower = gram[:HALF, :HALF], gram[HALF:, HALF:]
             r = lax.broadcasted_iota(jnp.int32, (HALF, HALF), 0)

time: 149 us -> 149 us (level)
  no operation moved by 1% of the time
where the time goes in v6:
time: 149 us
  blocking collectives  81.1 us (54%)
  Pallas kernels  66.7 us (45%)
    all_to_all x5, blocking collectives, exchange(): return lax.all_to_all(array, axis, split_axis=0, concat_axis=0, tiled=True)  81.1 us
    pallas_call x1, Pallas kernels, solve(): pl.pallas_call(functools.partial(solve_kernel, tokens), out_shape=[jax.Sh...  42.4 us
    pallas_call x1, Pallas kernels, build_sketches(): pl.pallas_call(functools.partial(sketch_kernel, math.sqrt(WIDTH / width))...  22 us

profile of v6, /device:TPU:0, one launch (start us, length us, event | category | flops | bytes accessed | tf_op | source)
XLA Modules:
  0.0 148.6 jit_solution(5868550443046915411)
XLA Ops:
  0.0 22.0 %sketch.1 = (bf16[512,4096]{1,0:T(8,128)(2,1)}, bf16[16,552,128]{2,1,0:T(8,128)(2,1)}, bf16[16,128,128]{2,1,0:T(8,128)(2,1)}, s32[1,1]{1,0:T(1,128)}) custom-call(s32[16,3584]{1,0:T(8,128)} %bitcast.15, bf16[512,3584]{1,0:T(8,128)(2,1)} %bitcast.14, bf16[512,4096]{1,0:T(8,128)(2,1)} %bitcast.13, s32[1,512]{1,0:T(1,128)} %bitcast.8, s32[1,64]{1,0:T(1,128)} %bitcast.10), custom_call_target="tpu_custom_call" | custom-call | tf_op jit(solution)/shard_map/sketch/pallas_call | solution.py:136
  22.0 0.0 copy-start.2
  22.7 0.0 copy-start
  22.7 38.6 %all_to_all.30.pack_ref = bf16[16,552,128]{2,1,0:T(8,128)(2,1)S(1)} all-to-all(bf16[16,552,128]{2,1,0:T(8,128)(2,1)} %get-tuple-element.18), channel_id=1, replica_groups=mesh['seq_0'=4,'seq_1'=4,'rep_0'=4,'rep_1'=2] {'seq_0','seq_1'}, dimensions={0} | all-to-all | bytes 4521984 | tf_op jit(solution)/shard_map/all_to_all | solution.py:364
  61.3 0.0 copy-done.2
  61.3 0.0 copy-start.1
  61.3 42.4 %solve.1 = (bf16[16,64,256]{2,1,0:T(8,128)(2,1)S(1)}, f32[8,128]{1,0:T(8,128)S(1)}) custom-call(bf16[16,552,128]{2,1,0:T(8,128)(2,1)S(1)} %all_to_all.30.pack_ref, s32[1,64]{1,0:T(1,128)S(1)} %bitcast.11, f32[64,256]{1,0:T(8,128)S(1)} %get-tuple-element.27.spare_ref), custom_call_target="tpu_custom_call" | custom-call | tf_op jit(solution)/shard_map/solve/pallas_call | solution.py:263
  103.7 13.9 %all_to_all.31.solved_ref = bf16[16,64,256]{2,1,0:T(8,128)(2,1)S(1)} all-to-all(bf16[16,64,256]{2,1,0:T(8,128)(2,1)S(1)} %get-tuple-element.21), channel_id=1, replica_groups=mesh['seq_0'=4,'seq_1'=4,'rep_0'=4,'rep_1'=2] {'seq_0','seq_1'}, dimensions={0} | all-to-all | bytes 1048576 | tf_op jit(solution)/shard_map/all_to_all | solution.py:364
  117.6 0.0 copy-done
  117.6 1.3 score.1
  118.9 10.2 %all_to_all.32.part_ref = f32[8,32,128]{2,1,0:T(8,128)S(1)} all-to-all(f32[8,32,128]{2,1,0:T(8,128)S(1)} %score.1), channel_id=1, replica_groups=mesh['seq_0'=4,'seq_1'=4,'rep_0'=4,'rep_1'=2] {'rep_0','rep_1'}, dimensions={0} | all-to-all | bytes 262144 | tf_op jit(solution)/shard_map/all_to_all | solution.py:364
  129.1 0.0 copy-done.1
  129.1 0.2 squares.1
  129.4 7.6 %all_to_all.33 = f32[8,1,128]{2,1,0:T(1,128)S(1)} all-to-all(f32[8,1,128]{2,1,0:T(1,128)S(1)} %broadcast_in_dim.16), channel_id=1, replica_groups=mesh['seq_0'=4,'seq_1'=4,'rep_0'=4,'rep_1'=2] {'rep_0','rep_1'}, dimensions={0} | all-to-all | bytes 8192 | tf_op jit(solution)/shard_map/all_to_all | solution.py:364
  137.0 10.8 %all_to_all.34.square_ref = f32[16,1,128]{2,1,0:T(1,128)S(1)} all-to-all(f32[16,1,128]{2,1,0:T(1,128)S(1)} %broadcast_in_dim.17), channel_id=1, replica_groups=mesh['seq_0'=4,'seq_1'=4,'rep_0'=4,'rep_1'=2] {'seq_0','seq_1'}, dimensions={0} | all-to-all | bytes 16384 | tf_op jit(solution)/shard_map/all_to_all | solution.py:364
  147.9 0.7 finish.1
  (5 shorter events, 0.1 us)
Async XLA Ops:
  22.0 39.3 %copy-start.2 = (s32[64]{0:T(128)S(1)}, s32[64]{0:T(128)}, u32[]{:S(2)}) copy-start(s32[64]{0:T(128)} %param.11) | copy-start | bytes 772
  22.7 94.9 %copy-start = (bf16[512,4096]{1,0:T(8,128)(2,1)S(1)}, bf16[512,4096]{1,0:T(8,128)(2,1)}, u32[]{:S(2)}) copy-start(bf16[512,4096]{1,0:T(8,128)(2,1)} %get-tuple-element.17.sketch_ref) | copy-start | bytes 12582916
  61.3 67.8 %copy-start.1 = (s32[512]{0:T(512)S(1)}, s32[512]{0:T(512)}, u32[]{:S(2)}) copy-start(s32[512]{0:T(512)} %param.10) | copy-start | bytes 6148

commit v7 on v6

--- a/solution.py
+++ b/solution.py
@@ -151,7 +151,7 @@
         ],
         out_shape=[
             pltpu.HBM((tokens, heads * WIDTH), BF16),
-            pltpu.HBM((heads, rows, HALF), BF16),
+            jax.ShapeDtypeStruct((heads, rows, HALF), BF16),
             pltpu.HBM((heads, 2 * queries, HALF), BF16),
             jax.ShapeDtypeStruct((1, 1), jnp.int32),
         ],

time: 149 us -> 148 us (level)
  no operation moved by 1% of the time
where the time goes in v7:
time: 148 us
  blocking collectives  80.9 us (55%)
  Pallas kernels  66.5 us (45%)
    all_to_all x5, blocking collectives, exchange(): return lax.all_to_all(array, axis, split_axis=0, concat_axis=0, tiled=True)  80.9 us
    pallas_call x1, Pallas kernels, solve(): pl.pallas_call(functools.partial(solve_kernel, tokens), out_shape=[jax.Sh...  42.4 us
    pallas_call x1, Pallas kernels, build_sketches(): pl.pallas_call(functools.partial(sketch_kernel, math.sqrt(WIDTH / width))...  21.8 us

profile of v7, /device:TPU:0, one launch (start us, length us, event | category | flops | bytes accessed | tf_op | source)
XLA Modules:
  0.0 148.1 jit_solution(17801688365994462593)
XLA Ops:
  0.0 21.8 %sketch.1 = (bf16[512,4096]{1,0:T(8,128)(2,1)}, bf16[16,552,128]{2,1,0:T(8,128)(2,1)S(1)}, bf16[16,128,128]{2,1,0:T(8,128)(2,1)}, s32[1,1]{1,0:T(1,128)}) custom-call(s32[16,3584]{1,0:T(8,128)} %bitcast.15, bf16[512,3584]{1,0:T(8,128)(2,1)} %bitcast.14, bf16[512,4096]{1,0:T(8,128)(2,1)} %bitcast.13, s32[1,512]{1,0:T(1,128)} %bitcast.8, s32[1,64]{1,0:T(1,128)} %bitcast.10), custom_call_target="tpu_custom_call" | custom-call | tf_op jit(solution)/shard_map/sketch/pallas_call | solution.py:136
  21.8 0.0 copy-start.2
  22.5 0.0 copy-start
  22.5 38.4 %all_to_all.30.pack_ref = bf16[16,552,128]{2,1,0:T(8,128)(2,1)S(1)} all-to-all(bf16[16,552,128]{2,1,0:T(8,128)(2,1)S(1)} %get-tuple-element.18), channel_id=1, replica_groups=mesh['seq_0'=4,'seq_1'=4,'rep_0'=4,'rep_1'=2] {'seq_0','seq_1'}, dimensions={0} | all-to-all | bytes 4521984 | tf_op jit(solution)/shard_map/all_to_all | solution.py:364
  60.9 0.0 copy-done.2
  60.9 0.0 copy-start.1
  60.9 42.4 %solve.1 = (bf16[16,64,256]{2,1,0:T(8,128)(2,1)S(1)}, f32[8,128]{1,0:T(8,128)S(1)}) custom-call(bf16[16,552,128]{2,1,0:T(8,128)(2,1)S(1)} %all_to_all.30.pack_ref, s32[1,64]{1,0:T(1,128)S(1)} %bitcast.11, f32[64,256]{1,0:T(8,128)S(1)} %get-tuple-element.27.spare_ref), custom_call_target="tpu_custom_call" | custom-call | tf_op jit(solution)/shard_map/solve/pallas_call | solution.py:263
  103.3 13.9 %all_to_all.31.solved_ref = bf16[16,64,256]{2,1,0:T(8,128)(2,1)S(1)} all-to-all(bf16[16,64,256]{2,1,0:T(8,128)(2,1)S(1)} %get-tuple-element.21), channel_id=1, replica_groups=mesh['seq_0'=4,'seq_1'=4,'rep_0'=4,'rep_1'=2] {'seq_0','seq_1'}, dimensions={0} | all-to-all | bytes 1048576 | tf_op jit(solution)/shard_map/all_to_all | solution.py:364
  117.2 0.0 copy-done
  117.2 1.3 score.1
  118.5 10.2 %all_to_all.32.part_ref = f32[8,32,128]{2,1,0:T(8,128)S(1)} all-to-all(f32[8,32,128]{2,1,0:T(8,128)S(1)} %score.1), channel_id=1, replica_groups=mesh['seq_0'=4,'seq_1'=4,'rep_0'=4,'rep_1'=2] {'rep_0','rep_1'}, dimensions={0} | all-to-all | bytes 262144 | tf_op jit(solution)/shard_map/all_to_all | solution.py:364
  128.7 0.0 copy-done.1
  128.7 0.2 squares.1
  128.9 7.6 %all_to_all.33 = f32[8,1,128]{2,1,0:T(1,128)S(1)} all-to-all(f32[8,1,128]{2,1,0:T(1,128)S(1)} %broadcast_in_dim.16), channel_id=1, replica_groups=mesh['seq_0'=4,'seq_1'=4,'rep_0'=4,'rep_1'=2] {'rep_0','rep_1'}, dimensions={0} | all-to-all | bytes 8192 | tf_op jit(solution)/shard_map/all_to_all | solution.py:364
  136.6 10.8 %all_to_all.34.square_ref = f32[16,1,128]{2,1,0:T(1,128)S(1)} all-to-all(f32[16,1,128]{2,1,0:T(1,128)S(1)} %broadcast_in_dim.17), channel_id=1, replica_groups=mesh['seq_0'=4,'seq_1'=4,'rep_0'=4,'rep_1'=2] {'seq_0','seq_1'}, dimensions={0} | all-to-all | bytes 16384 | tf_op jit(solution)/shard_map/all_to_all | solution.py:364
  147.4 0.7 finish.1
  (5 shorter events, 0.1 us)
Async XLA Ops:
  21.8 39.1 %copy-start.2 = (s32[64]{0:T(128)S(1)}, s32[64]{0:T(128)}, u32[]{:S(2)}) copy-start(s32[64]{0:T(128)} %param.11) | copy-start | bytes 772
  22.5 94.7 %copy-start = (bf16[512,4096]{1,0:T(8,128)(2,1)S(1)}, bf16[512,4096]{1,0:T(8,128)(2,1)}, u32[]{:S(2)}) copy-start(bf16[512,4096]{1,0:T(8,128)(2,1)} %get-tuple-element.17.sketch_ref) | copy-start | bytes 12582916
  60.9 67.8 %copy-start.1 = (s32[512]{0:T(512)S(1)}, s32[512]{0:T(512)}, u32[]{:S(2)}) copy-start(s32[512]{0:T(512)} %param.10) | copy-start | bytes 6148
